TPU v7x, 8 devices: a whole 2x2x1 slice. The times are simulated.
8 devices in a mesh: dp: 1 (over z), fsdp: 8 (over y, x, core).
Axes of the slice: x: 2, y: 2, z: 1, core: 2. Of those that a mesh axis runs over, the one named last changes fastest.
Arguments:
- tok_ids: int32 [48, 384], P(('dp', 'fsdp'))
- grad_out: bfloat16 [48, 384, 2048], P(('dp', 'fsdp'))
- emb_table: bfloat16 [163840, 2048], P('fsdp')
- norm_gain: bfloat16 [2048], P('fsdp')
- w_query: bfloat16 [2048, 3072], P('fsdp')
- w_kv_down: bfloat16 [2048, 576], P('fsdp')
- kv_gain: bfloat16 [512], P('fsdp')
- w_kv_up: bfloat16 [512, 4096], P('fsdp')
- w_out: bfloat16 [2048, 2048], P('fsdp')
Outputs:
- output 1: bfloat16 [48, 384, 2048], P(('dp', 'fsdp'))
- output 2: bfloat16 [163840, 2048], P(('dp', 'fsdp'))
- output 3: float32 [2048], P(('dp', 'fsdp'))
- output 4: float32 [2048, 3072], P(('dp', 'fsdp'))
- output 5: float32 [2048, 576], P(('dp', 'fsdp'))
- output 6: float32 [512], P(('dp', 'fsdp'))
- output 7: float32 [512, 4096], P(('dp', 'fsdp'))
- output 8: float32 [2048, 2048], P(('dp', 'fsdp'))
All inputs are finite; a program needn't handle non-finite values.
Results may differ from a plain program's by a relative error of at most 0.011954.
Values are sent between devices in bfloat16 or wider.
A program may use at most 1 GiB of HBM per device.

v0:
```python
import functools
import math
import jax
import jax.numpy as jnp
import numpy as np
from jax import lax
from jax.experimental import pallas as pl
from jax.experimental.pallas import tpu as pltpu
from jax.sharding import PartitionSpec as P

NOPE_DIM = 128
ROPE_DIM = 64
VALUE_DIM = 128
ROPE_THETA = 50000.0
RMS_EPS = 1e-6
ATTN_SCALE = (NOPE_DIM + ROPE_DIM) ** -0.5 * (0.1 * math.log(32.0) + 1.0) ** 2
ROW_DIMS = (((0,), (0,)), ((), ()))
COL_DIMS = (((1,), (1,)), ((), ()))
LANES = 128
HALVES = 2
PAIR = 2 * LANES
TABLE_BLOCK = 1024
CHUNK = 16
GROUP = 16
ADD_RING = 4
UNROLL = 8
NO_ROW = 1 << 30
PITCH = 17
F32 = jnp.float32
BF16 = jnp.bfloat16
SMEM = pltpu.SMEM
ANY = pl.ANY
HBM = pl.BlockSpec(memory_space=ANY)
SCALARS = pl.BlockSpec(memory_space=SMEM)


def step_id():
    return pl.program_id(0)


def last_step():
    return pl.program_id(0) == pl.num_programs(0) - 1


def shift_of(x, n):
    return lax.shift_right_logical(x, n.bit_length() - 1)


def lane(j, n=1):
    return slice(j * LANES, (j + n) * LANES)


def low_lanes():
    return lax.broadcasted_iota(jnp.int32, (1, LANES), 1) < ROPE_DIM


def rotate(x, n):
    return pltpu.roll(x, n, 1)


def column(g, j):
    return pl.ds(g * GROUP * PITCH + j, GROUP, stride=PITCH)


def group(g):
    return pl.ds(g * GROUP, GROUP)


def rowsum(x):
    return jnp.sum(x, axis=-1, keepdims=True)


def tree_sum(terms):
    while len(terms) > 1:
        terms = [a + b for a, b in zip(terms[::2], terms[1::2])]
    return terms[0]


def inverse_rms(square_sum, width):
    return lax.rsqrt(square_sum * (1.0 / width) + RMS_EPS)


def row_spec(blk, width):
    return pl.BlockSpec((blk, width), lambda i, *_: (i, 0))


def whole_spec(shape, **kw):
    return pl.BlockSpec(shape, lambda *_: (0,) * len(shape), **kw)


def struct(shape, dtype):
    return jax.ShapeDtypeStruct(shape, dtype)


def cost(flops, size):
    return pl.CostEstimate(flops=int(flops), bytes_accessed=int(size), transcendentals=0)


CHEAP = cost(6e7, 1e7)
SMALL, LARGE, FULL = 40, 48, 62


def params(vmem_mib, **kw):
    return pltpu.CompilerParams(vmem_limit_bytes=vmem_mib << 20, **kw)


def unique_body(shift, halves, keys_ref, uniq_ref, rank_ref, count_ref):
    n = keys_ref.shape[0] // halves
    for h in range(halves):
        def step(i, carry):
            k, prev = carry
            for j in range(UNROLL):
                key = keys_ref[h * n + i * UNROLL + j]
                row = lax.shift_right_logical(key, shift)
                k = k + (row != prev).astype(jnp.int32)
                uniq_ref[h * n + k] = row
                rank_ref[h * n + (key & ((1 << shift) - 1))] = k
                prev = row
            return k, prev

        k, _ = lax.fori_loop(0, n // UNROLL, step, (jnp.int32(-1), jnp.int32(-1)))
        count_ref[h] = k + 1


def unique_rows(ids):
    halves, n = ids.shape
    shift = (n - 1).bit_length()
    keys = lax.sort(ids * (1 << shift) + jnp.arange(n, dtype=jnp.int32), dimension=1)
    flat = struct((halves * n,), jnp.int32)
    uniq, rank, count = pl.pallas_call(
        functools.partial(unique_body, shift, halves), out_shape=[flat, flat, struct((halves,), jnp.int32)],
        in_specs=[SCALARS], out_specs=[SCALARS] * 3, name="unique_rows")(keys.reshape(-1))
    known = jnp.arange(n, dtype=jnp.int32) < count[:, None]
    return jnp.where(known, uniq.reshape(halves, n), NO_ROW), rank.reshape(halves, n)


def pick_body(n_list, n_dev, n_tok, base, extra, rows_ref, edge_ref, table_ref, *refs):
    halves = n_list // n_dev
    base_refs, extra_refs, (lin_ref, stage_ref, sems) = refs[:halves], refs[halves:-3], refs[-3:]
    b = step_id()
    last = last_step()
    rows_blk, d_model = table_ref.shape
    cols = d_model // LANES
    n_edge = edge_ref.shape[0] // n_list

    def chunk_copies(l, k, act):
        src, sem, at = stage_ref.at[l, pl.ds(k * CHUNK, CHUNK)], sems.at[l, k], k * CHUNK

        @pl.when(at < base)
        def _():
            getattr(pltpu.make_async_copy(src, base_refs[l // n_dev].at[pl.ds(l % n_dev * base + at, CHUNK)], sem), act)()

        if extra:
            @pl.when(at >= base)
            def _():
                getattr(pltpu.make_async_copy(src, extra_refs[l].at[pl.ds(at - base, CHUNK)], sem), act)()

    @pl.loop(0, rows_blk // GROUP)
    def _(g):
        for j in range(cols):
            lin_ref[column(g, j), :] = table_ref[group(g), lane(j)].astype(F32)

    origin = b * (rows_blk * PITCH)
    for l in range(n_list):
        first = edge_ref[l * n_edge]
        lo = jnp.minimum(edge_ref[l * n_edge + b] - first, base + extra)
        hi = jnp.minimum(edge_ref[l * n_edge + b + 1] - first, base + extra)
        at = l * n_tok + first

        @pl.loop(0, shift_of(hi - lo + UNROLL - 1, UNROLL))
        def _(i):
            p = lo + i * UNROLL
            vals = [lin_ref[pl.ds(jnp.minimum(rows_ref[at + p + u] - origin, (rows_blk - 1) * PITCH), cols), :] for u in range(UNROLL)]
            for u in range(UNROLL):
                stage_ref[l, p + u] = vals[u].astype(BF16)

        @pl.loop(shift_of(lo, CHUNK), jnp.where(last, shift_of(hi + CHUNK - 1, CHUNK), shift_of(hi, CHUNK)))
        def _(k):
            chunk_copies(l, k, 'start')

    @pl.when(last)
    def _():
        for l in range(n_list):
            total = jnp.minimum(edge_ref[(l + 1) * n_edge - 1] - edge_ref[l * n_edge], base + extra)

            @pl.loop(0, shift_of(total + CHUNK - 1, CHUNK))
            def _(k):
                chunk_copies(l, k, 'wait')


def row_spots(rows):
    return jnp.pad(jnp.minimum(rows, NO_ROW // PITCH).reshape(-1) * PITCH, (0, UNROLL))


def pick_rows(table, rows, edges, n_dev, base, extra):
    n_list, n_tok = rows.shape
    n_rows, d_model = table.shape
    cols = d_model // LANES
    out = [struct((n_dev * base, cols, LANES), BF16)] * (n_list // n_dev) + [struct((extra, cols, LANES), BF16)] * (n_list if extra else 0)
    return pl.pallas_call(
        functools.partial(pick_body, n_list, n_dev, n_tok, base, extra),
        grid_spec=pltpu.PrefetchScalarGridSpec(
            num_scalar_prefetch=2, grid=(n_rows // TABLE_BLOCK,), in_specs=[row_spec(TABLE_BLOCK, d_model)], out_specs=[HBM] * len(out),
            scratch_shapes=[
                pltpu.VMEM((TABLE_BLOCK * PITCH, LANES), F32),
                pltpu.VMEM((n_list, base + extra + UNROLL, cols, LANES), BF16),
                pltpu.SemaphoreType.DMA((n_list, (base + extra) // CHUNK))]),
        out_shape=out, compiler_params=params(FULL), name="pick_rows", cost_estimate=CHEAP,
    )(row_spots(rows), edges.reshape(-1), table)


def spread_body(pieces, rank_ref, slot_ref, gain_ref, *refs):
    piece_refs, (h0_ref, x_ref, lin_ref, recv_ref, sems) = refs[:len(pieces)], refs[len(pieces):]
    i = step_id()
    rows_blk, d_model = h0_ref.shape
    cols = d_model // LANES

    @pl.when(i == 0)
    def _():
        for act in ('start', 'wait'):
            for n, (to, size, device) in enumerate(pieces):
                @pl.when((lax.axis_index('fsdp') == device) if device is not None else (i == 0))
                def _():
                    getattr(pltpu.make_async_copy(piece_refs[n], recv_ref.at[pl.ds(to, size)], sems.at[n]), act)()

    @pl.loop(0, rows_blk // UNROLL)
    def _(t0):
        for u in range(UNROLL):
            t = t0 * UNROLL + u
            lin_ref[pl.ds(t * PITCH, cols), :] = recv_ref[slot_ref[rank_ref[i * rows_blk + t]]].astype(F32)

    @pl.loop(0, rows_blk // (HALVES * GROUP))
    def _(g):
        groups = []
        for u in range(HALVES):
            tiles = [lin_ref[column(2 * g + u, j), :] for j in range(cols)]
            groups.append((tiles, rowsum(tree_sum([v * v for v in tiles]))))
        for u, (tiles, square) in enumerate(groups):
            inv = inverse_rms(square, d_model)
            for j, v in enumerate(tiles):
                at = (group(2 * g + u), lane(j))
                h0_ref[at] = v.astype(BF16)
                x_ref[at] = (v * inv * gain_ref[:, lane(j)]).astype(BF16)


def spread_rows(pieces, rank, slot, gain, n_slots):
    n_tok, d_model = rank.shape[0], gain.shape[0]
    cols = d_model // LANES
    blk = 128
    rows = row_spec(blk, d_model)
    plan = [(to, v.shape[0], device) for v, to, device in pieces]
    return pl.pallas_call(
        functools.partial(spread_body, plan),
        grid_spec=pltpu.PrefetchScalarGridSpec(
            num_scalar_prefetch=2, grid=(n_tok // blk,), in_specs=[whole_spec((1, d_model))] + [HBM] * len(pieces), out_specs=[rows, rows],
            scratch_shapes=[pltpu.VMEM((blk * PITCH, LANES), F32), pltpu.VMEM((n_slots, cols, LANES), BF16), pltpu.SemaphoreType.DMA((len(pieces),))]),
        out_shape=[struct((n_tok, d_model), BF16)] * 2, compiler_params=params(SMALL), name="spread_rows",
        cost_estimate=CHEAP,
    )(rank, slot, gain.reshape(1, d_model), *[v for v, _, _ in pieces])


def rope_tables(seq_len):
    pos = np.arange(seq_len, dtype=np.float32)
    inv_freq = (np.float32(ROPE_THETA) ** (np.float32(-2.0) * np.arange(ROPE_DIM // 2, dtype=np.float32) / np.float32(ROPE_DIM))).astype(np.float32)
    angle = (pos[:, None] * inv_freq[None, :]).astype(np.float32).astype(np.float64)
    cos, sin, zero = np.cos(angle), np.sin(angle), np.zeros_like(angle)
    full = lambda lo, hi: np.concatenate([lo, hi, lo, hi], axis=1).astype(np.float32)
    return full(cos, cos), full(-sin, zero), full(zero, sin)


def turn(vals, cos, sin_lo, sin_hi, sign=1.0):
    half = ROPE_DIM // 2
    return vals * cos + sign * (rotate(vals, LANES - half) * sin_lo + rotate(vals, half) * sin_hi)


def attn_body(q_ref, pe_ref, kv_ref, do_ref, cos_ref, sin_lo_ref, sin_hi_ref,
              o_ref, dq_ref, dkv_ref, dpe_ref, krot_ref, qcat_ref, p_ref, ds_ref, dkrot_ref):
    pair = pl.program_id(1)
    seq_len = q_ref.shape[0]
    blk = 128
    n_blk = seq_len // blk
    low = low_lanes()

    @pl.when(pair == 0)
    def _():
        pe = pe_ref[:].astype(F32)
        pe = jnp.where(low, pe, rotate(pe, ROPE_DIM))
        krot_ref[:] = turn(pe, cos_ref[:], sin_lo_ref[:], sin_hi_ref[:]).astype(BF16)
        dkrot_ref[:] = jnp.zeros_like(dkrot_ref)

    qrot = turn(q_ref[:, PAIR:].astype(F32), cos_ref[:], sin_lo_ref[:], sin_hi_ref[:])
    for h in range(HALVES):
        mine = low if h == 0 else ~low
        qcat_ref[h, :, :LANES] = q_ref[:, lane(h)]
        qcat_ref[h, :, LANES:] = jnp.where(mine, qrot, 0.0).astype(BF16)
    causal = lax.broadcasted_iota(jnp.int32, (blk, blk), 0) >= lax.broadcasted_iota(jnp.int32, (blk, blk), 1)
    blocks = [(h, i, slice(i * blk, (i + 1) * blk), (i + 1) * blk) for i in reversed(range(n_blk)) for h in range(HALVES)]
    key = lambda h: lane(2 * h)
    val = lambda h: lane(2 * h + 1)
    head = lane
    kcat = lambda h, seen: jnp.concatenate([kv_ref[:seen, key(h)], krot_ref[:seen]], axis=1)
    scores = [lax.dot_general(qcat_ref[h, here], kcat(h, seen), COL_DIMS, preferred_element_type=F32) for h, i, here, seen in blocks]
    dps = [lax.dot_general(do_ref[here, head(h)], kv_ref[:seen, val(h)], COL_DIMS, preferred_element_type=F32) for h, i, here, seen in blocks]
    for (h, i, here, seen), s, dp in zip(blocks, scores, dps):
        diag = jnp.where(causal, s[:, i * blk:], -1e30)
        s = diag if i == 0 else jnp.concatenate([s[:, :i * blk], diag], axis=1)
        e = jnp.exp2((s - jnp.max(s, axis=-1, keepdims=True)) * (ATTN_SCALE * math.log2(math.e)))
        p = e * (1.0 / rowsum(e))
        p_ref[h, here, :seen] = p.astype(BF16)
        ds_ref[h, here, :seen] = (p * (dp - rowsum(dp * p)) * ATTN_SCALE).astype(BF16)
    dqrots = [[], []]
    for h, i, here, seen in blocks:
        o_ref[here, head(h)] = jnp.dot(p_ref[h, here, :seen], kv_ref[:seen, val(h)], preferred_element_type=F32).astype(BF16)
        dqi = jnp.dot(ds_ref[h, here, :seen], kcat(h, seen), preferred_element_type=F32)
        dq_ref[here, head(h)] = dqi[:, :LANES].astype(BF16)
        dqrots[h].append(dqi[:, LANES:])
    for h in range(HALVES):
        for j in range(n_blk):
            here, later = slice(j * blk, (j + 1) * blk), slice(j * blk, seq_len)
            dv = lax.dot_general(p_ref[h, later, here], do_ref[later, head(h)], ROW_DIMS, preferred_element_type=F32)
            dk = lax.dot_general(ds_ref[h, later, here], qcat_ref[h, later], ROW_DIMS, preferred_element_type=F32)
            dkv_ref[here, val(h)] = dv.astype(BF16)
            dkv_ref[here, key(h)] = dk[:, :LANES].astype(BF16)
            dkrot_ref[here] += dk[:, LANES:]
    for n, i in enumerate(reversed(range(n_blk))):
        here = slice(i * blk, (i + 1) * blk)
        dqr = jnp.where(low, dqrots[0][n], dqrots[1][n]).astype(BF16).astype(F32)
        dq_ref[here, PAIR:] = turn(dqr, cos_ref[here], sin_lo_ref[here], sin_hi_ref[here], -1.0).astype(BF16)

    @pl.when(pair == pl.num_programs(1) - 1)
    def _():
        both = dkrot_ref[:]
        both = (both + rotate(both, ROPE_DIM)).astype(BF16).astype(F32)
        dpe = turn(both, cos_ref[:], sin_lo_ref[:], sin_hi_ref[:], -1.0)
        dpe_ref[:] = jnp.where(low, dpe, 0.0).astype(BF16)


def attend(qx, kv, d_mix, first_seq, seq_count, pe_block):
    tok = qx.shape[0]
    seq_len = tok // seq_count
    pairs = d_mix.shape[1] // (2 * VALUE_DIM)
    tabs = [jnp.asarray(t) for t in rope_tables(seq_len)]
    at = lambda width: pl.BlockSpec((seq_len, width), lambda s, j: (s, j))
    tab = whole_spec((seq_len, LANES))
    shape = lambda w: struct((tok, w), BF16)
    return pl.pallas_call(
        attn_body, grid=(seq_count, pairs),
        in_specs=[at(3 * LANES), pl.BlockSpec((seq_len, LANES), lambda s, j: (s, pe_block)), at(4 * LANES), pl.BlockSpec((seq_len, PAIR), lambda s, j: (s + first_seq, j)), tab, tab, tab],
        out_specs=[at(PAIR), at(3 * LANES), at(4 * LANES), pl.BlockSpec((seq_len, LANES), lambda s, j: (s, 0))],
        out_shape=[shape(pairs * PAIR), shape(qx.shape[1]), shape(pairs * 4 * LANES), shape(LANES)],
        scratch_shapes=[pltpu.VMEM((seq_len, LANES), BF16), pltpu.VMEM((2, seq_len, PAIR), BF16),
                        pltpu.VMEM((2, seq_len, seq_len), BF16), pltpu.VMEM((2, seq_len, seq_len), BF16),
                        pltpu.VMEM((seq_len, LANES), F32)],
        compiler_params=params(SMALL), name="attention",
        cost_estimate=cost(qx.size * tok, qx.size),
    )(qx, qx, kv, d_mix, *tabs)


def latent_body(w_ref, c_ref, pe_ref, gain_ref, _, out_ref, dgain_ref, gacc_ref):
    i = step_id()
    rank = gain_ref.shape[1]

    @pl.when(i == 0)
    def _():
        gacc_ref[:] = jnp.zeros_like(gacc_ref)

    c = c_ref[:].astype(F32)
    w = w_ref[:].astype(F32)
    inv = inverse_rms(rowsum(c * c), rank)
    hat = c * inv
    gacc_ref[:] += jnp.sum((w * hat).reshape(-1, 8, rank), axis=0)
    w = w * gain_ref[:]
    out_ref[:, :rank] = (inv * (w - hat * (rowsum(w * hat) / rank))).astype(BF16)
    out_ref[:, rank:] = pe_ref[:]

    @pl.when(last_step())
    def _():
        dgain_ref[:] = jnp.sum(gacc_ref[:], axis=0, keepdims=True)


def latent_back(d_latent, qx, d_pe, gain, d_qx, latent_at):
    tok, rank = d_latent.shape
    blk = 3 * LANES
    wide = lambda width, at: pl.BlockSpec((pl.Element(blk), pl.Element(width)), lambda i: (i * blk, at))
    return pl.pallas_call(
        latent_body, grid=(tok // blk,),
        in_specs=[row_spec(blk, rank), wide(rank, latent_at), row_spec(blk, LANES), whole_spec((1, rank)), HBM],
        out_specs=[wide(rank + LANES, latent_at), whole_spec((1, rank))],
        out_shape=[struct(d_qx.shape, BF16), struct((1, rank), F32)],
        scratch_shapes=[pltpu.VMEM((8, rank), F32)], input_output_aliases={4: 0}, name="latent_back",
        cost_estimate=CHEAP,
    )(d_latent, qx, d_pe, gain.reshape(1, rank), d_qx)


def merge_body(rank_ref, slot_ref, dx_ref, h0_ref, dy_ref, gain_ref, base_ref, extra_ref, dgain_ref, even_ref, odd_ref, acc_ref, gacc_ref, sem):
    i = step_id()
    rows_blk, d_model = h0_ref.shape
    cols = d_model // LANES

    @pl.when(i == 0)
    def _():
        gacc_ref[:] = jnp.zeros_like(gacc_ref)

        @pl.loop(0, acc_ref.shape[0] // 8)
        def _(r):
            acc_ref[pl.ds(r * 8, 8)] = jnp.zeros((8,) + acc_ref.shape[1:], F32)

    lanes = [lane(j) for j in range(cols)]

    def derive(g, lin_ref):
        rows = group(g)
        squares, crosses = [], []
        for at in lanes:
            v = h0_ref[rows, at].astype(F32)
            squares.append(v * v)
            crosses.append(v * (dx_ref[rows, at].astype(F32) * gain_ref[:, at]))
        inv = inverse_rms(rowsum(tree_sum(squares)), d_model)
        mean = rowsum(tree_sum(crosses)) * inv / d_model
        for j, at in enumerate(lanes):
            hat = h0_ref[rows, at].astype(F32) * inv
            w = dx_ref[rows, at].astype(F32)
            gacc_ref[:, at] += w * hat
            lin_ref[column(0, j), :] = inv * (w * gain_ref[:, at] - hat * mean) + dy_ref[rows, at].astype(F32)

    def add(g, lin_ref):
        for t in range(GROUP):
            r = slot_ref[rank_ref[i * rows_blk + g * GROUP + t]]
            acc_ref[r] = acc_ref[r] + lin_ref[pl.ds(t * PITCH, cols), :]

    derive(0, even_ref)
    pairs = rows_blk // (HALVES * GROUP)

    @pl.loop(0, pairs - 1)
    def _(g):
        add(2 * g, even_ref)
        derive(2 * g + 1, odd_ref)
        add(2 * g + 1, odd_ref)
        derive(2 * g + 2, even_ref)

    add(2 * pairs - 2, even_ref)
    derive(2 * pairs - 1, odd_ref)
    add(2 * pairs - 1, odd_ref)

    @pl.when(last_step())
    def _():
        dgain_ref[:] = jnp.sum(gacc_ref[:], axis=0, keepdims=True)
        split = base_ref.shape[0]
        copies = [pltpu.make_async_copy(acc_ref.at[pl.ds(0, split)], base_ref, sem.at[0]),
                  pltpu.make_async_copy(acc_ref.at[pl.ds(split, extra_ref.shape[0])], extra_ref, sem.at[1])]
        for copy in copies:
            copy.start()
        for copy in copies:
            copy.wait()


def merge_rows(dx, h0, dy, dy_at, gain, rank, slot, base, extra):
    n_tok, d_model = h0.shape
    cols = d_model // LANES
    blk = 128
    rows = row_spec(blk, d_model)
    return pl.pallas_call(
        merge_body,
        grid_spec=pltpu.PrefetchScalarGridSpec(
            num_scalar_prefetch=2, grid=(n_tok // blk,),
            in_specs=[rows, rows, pl.BlockSpec((blk, d_model), lambda i, *_: (i + dy_at // blk, 0)), whole_spec((1, d_model))],
            out_specs=[HBM, HBM, whole_spec((1, d_model))],
            scratch_shapes=[pltpu.VMEM((GROUP * PITCH, LANES), F32)] * 2 + [ pltpu.VMEM((base + extra, cols, LANES), F32),
                            pltpu.VMEM((GROUP, d_model), F32), pltpu.SemaphoreType.DMA((2,))]),
        out_shape=[struct((base, cols, LANES), F32), struct((extra, cols, LANES), F32), struct((1, d_model), F32)],
        compiler_params=params(SMALL), name="merge_rows",
        cost_estimate=CHEAP,
    )(rank, slot, dx, h0, dy, gain.reshape(1, d_model))


def add_body(n_dev, n_tok, halves, rows_ref, edge_ref, *refs):
    flat, (out_ref, acc_ref, ring_ref, sems) = list(refs[:-4]), refs[-4:]
    sources = []
    for stride, base, extras in halves:
        first = flat.pop(0)
        more = [[flat.pop(0) for _ in range(n)] for n in extras]
        sources += [(first, d * stride, base, more[d] if extras else []) for d in range(n_dev)]
    b = step_id()
    n_blk = pl.num_programs(0)
    rows_blk, d_model = out_ref.shape
    cols = d_model // LANES
    n_edge = edge_ref.shape[0] // len(sources)
    size, ring = CHUNK, ADD_RING

    def landing(s, k):
        return ring_ref.at[s, pl.ds((k & (ring - 1)) * size, size)], sems.at[s, k & (ring - 1)]

    def chunk_start(s, k):
        first, at, base, more = sources[s]
        dst, sem = landing(s, k)

        @pl.when(k * size < base)
        def _():
            pltpu.make_async_copy(first.at[pl.ds(at + k * size, size)], dst, sem).start()

        for ref in more:
            @pl.when((k * size >= base) & (k * size < base + ref.shape[0]))
            def _():
                pltpu.make_async_copy(ref.at[pl.ds(k * size - base, size)], dst, sem).start()

            base = base + ref.shape[0]

    def chunk_wait(s, k):
        dst, sem = landing(s, k)
        pltpu.make_async_copy(sources[s][0].at[pl.ds(0, size)], dst, sem).wait()

    def chunks_of(s):
        return shift_of(edge_ref[s * n_edge + n_blk] - edge_ref[s * n_edge] + size - 1, size)

    @pl.when(b == 0)
    def _():
        for s in range(len(sources)):
            @pl.loop(0, jnp.minimum(chunks_of(s), ring))
            def _(k):
                chunk_start(s, k)

    @pl.loop(0, rows_blk // GROUP)
    def _(r):
        for u in range(HALVES * PITCH):
            acc_ref[pl.ds((r * HALVES * PITCH + u) * 8, 8), :] = jnp.zeros((8, LANES), F32)

    for s in range(len(sources)):
        first = edge_ref[s * n_edge]
        lo = edge_ref[s * n_edge + b] - first
        hi = edge_ref[s * n_edge + b + 1] - first
        at = s * n_tok + first
        origin = b * (rows_blk * PITCH)

        @pl.when(hi > lo)
        def _():
            @pl.loop(shift_of(lo, size), shift_of(hi - 1, size) + 1)
            def _(k):
                start = jnp.maximum(lo, k * size)
                stop = jnp.minimum(hi, (k + 1) * size)

                @pl.when(start == k * size)
                def _():
                    chunk_wait(s, k)

                @pl.loop(0, shift_of(stop - start + UNROLL - 1, UNROLL))
                def _(i):
                    p = start + i * UNROLL
                    spots, sums = [], []
                    for u in range(UNROLL):
                        spots.append(pl.ds(jnp.where(p + u < stop, rows_ref[at + p + u] - origin, rows_blk * PITCH), cols))
                        sums.append(acc_ref[spots[u], :] + ring_ref[s, (p + u) & (ring * size - 1)])
                    for u in range(UNROLL):
                        acc_ref[spots[u], :] = sums[u]

                @pl.when((stop == (k + 1) * size) & (k + ring < chunks_of(s)))
                def _():
                    chunk_start(s, k + ring)

    @pl.loop(0, rows_blk // GROUP)
    def _(g):
        for j in range(cols):
            out_ref[group(g), lane(j)] = acc_ref[column(g, j), :].astype(BF16)


def add_rows(halves, rows, edges, n_dev, n_rows):
    n_list, n_tok = rows.shape
    cols = halves[0][0].shape[1]
    d_model = cols * LANES
    runs = [[v if isinstance(v, tuple) else (v,) for v in more] for *_, more in halves]
    arrays = [v for half, more in zip(halves, runs) for v in [half[0]] + [u for run in more for u in run]]
    block = HALVES * TABLE_BLOCK
    edges = edges[:, ::HALVES]
    return pl.pallas_call(
        functools.partial(add_body, n_dev, n_tok, [(stride, base, [len(run) for run in more]) for (_, stride, base, _), more in zip(halves, runs)]),
        grid_spec=pltpu.PrefetchScalarGridSpec(
            num_scalar_prefetch=2, grid=(n_rows // block,), in_specs=[HBM] * len(arrays), out_specs=row_spec(block, d_model),
            scratch_shapes=[pltpu.VMEM(((block + 1) * PITCH, LANES), F32),
                            pltpu.VMEM((n_list, ADD_RING * CHUNK, cols, LANES), F32),
                            pltpu.SemaphoreType.DMA((n_list, ADD_RING))]),
        out_shape=struct((n_rows, d_model), BF16), compiler_params=params(FULL), name="add_rows", cost_estimate=CHEAP,
    )(row_spots(rows), edges.reshape(-1), *arrays)


def exchange_body(base, n_extra, n_dev, base_ref, *refs):
    extra_refs, (lhs_ref, rhs_ref, out_ref, via_ref, prod_ref, send_sems, recv_sems, hop_send, hop_recv, end_send, end_recv, own_sems) = refs[:n_extra], refs[n_extra:]
    place = lax.axis_index('fsdp')
    far, side = n_dev - 2, n_dev // 2
    across = lambda m: [((m ^ far) & ~1) | c for c in range(HALVES)]

    def moves(src, dst):
        runs = [(0, base_ref, dst * base, src * base, base)]
        if n_extra and src == 0:
            runs.append((1, extra_refs[dst], 0, n_dev * base, extra_refs[dst].shape[0]))
        out = []
        for kind, ref, at, to, n in runs:
            by = 0 if (src ^ dst) & far != far else (n // 2, n, 0, n // 2)[src >> 1]
            out.append((kind, ref, at, to, n - by, by))
        return out

    def remote(src, dst, send, recv, to):
        return pltpu.make_async_remote_copy(src, dst, send, recv, device_id={'fsdp': to}, device_id_type=pl.DeviceIdType.MESH)

    def direct(src, dst):
        return [remote(ref.at[pl.ds(at, n)], out_ref.at[pl.ds(to, n)], send_sems.at[kind * n_dev + dst], recv_sems.at[kind * n_dev + src], dst)
                for kind, ref, at, to, n, _ in moves(src, dst) if n]

    def hop(src, dst):
        out = []
        for kind, ref, at, _, n, by in moves(src, dst):
            lot = HALVES * kind + (dst & 1)
            if by:
                out.append(remote(ref.at[pl.ds(at + n, by)], via_ref.at[lot, pl.ds(0, by)], hop_send.at[lot], hop_recv.at[lot], src ^ side))
        return out

    def end(src, dst):
        return [remote(via_ref.at[HALVES * kind + (dst & 1), pl.ds(0, by)], out_ref.at[pl.ds(to + n, by)], end_send.at[HALVES * kind + (dst & 1)], end_recv.at[HALVES * kind + (src & 1)], dst)
                for kind, _, _, to, n, by in moves(src, dst) if by]

    def own(m):
        return [pltpu.make_async_copy(ref.at[pl.ds(at, n)], out_ref.at[pl.ds(to, n)], own_sems.at[kind]) for kind, ref, at, to, n, _ in moves(m, m)]

    each = lambda copies, act: [getattr(c, act)() for c in copies]

    @pl.when(step_id() == 0)
    def _():
        for m in range(n_dev):
            @pl.when(place == m)
            def _():
                for dst in across(m):
                    each(hop(m, dst), 'start')
                for k in reversed(range(1, n_dev)):
                    each(direct(m, m ^ k), 'start')
                each(own(m), 'start')

    for n in range(0, prod_ref.shape[1], PAIR * HALVES):
        cols = slice(n, n + PAIR * HALVES)
        prod_ref[:, cols] = lax.dot_general(lhs_ref[:], rhs_ref[cols], COL_DIMS, preferred_element_type=F32).astype(BF16)

    @pl.when(last_step())
    def _():
        for m in range(n_dev):
            @pl.when(place == m)
            def _():
                for dst in across(m ^ side):
                    each(hop(m ^ side, dst), 'wait_recv')
                    each(end(m ^ side, dst), 'start')
                each(own(m), 'wait')
                for dst in across(m):
                    each(hop(m, dst), 'wait_send')
                for k in range(1, n_dev):
                    each(direct(m, m ^ k), 'wait_send')
                    each(direct(m ^ k, m), 'wait_recv')
                for dst in across(m ^ side):
                    each(end(m ^ side, dst), 'wait_send')
                for src in across(m):
                    each(end(src, m), 'wait_recv')


def exchange(base_rows, extras, n_dev, lhs, rhs):
    rows, *cols = base_rows.shape
    base, extra = rows // n_dev, extras[0].shape[0] if extras else 0
    quad, pair = (pltpu.SemaphoreType.DMA((n,)) for n in (4, HALVES * n_dev))
    near = (rhs.shape[0], lhs.shape[1])
    shapes = [(rows + extra, *cols), (4, max(base, extra), *cols), (lhs.shape[0], near[0])]
    return pl.pallas_call(
        functools.partial(exchange_body, base, len(extras), n_dev), grid=(lhs.shape[0] // PAIR,), out_shape=[struct(v, BF16 if v == shapes[-1] else base_rows.dtype) for v in shapes],
        in_specs=[HBM] * (len(extras) + 1) + [row_spec(PAIR, near[1]), whole_spec(near, pipeline_mode=pl.Buffered(1))], out_specs=[HBM, HBM, row_spec(PAIR, near[0])],
        scratch_shapes=[pair, pair, quad, quad, quad, quad, quad],
        compiler_params=params(SMALL, has_side_effects=True), name="exchange", cost_estimate=cost(lhs.size * lhs.size, lhs.size),
    )(base_rows, *extras, lhs, rhs)[::HALVES]


def fetch_beside(base, extras):
    got = base_beside(base)
    more = [v if d == 0 else lax.ppermute(v, 'fsdp', [(0, d)]) for d, v in enumerate(extras)]
    return [got] + more


def bring_beside(extra, n_dev):
    last = n_dev - 1
    cut = extra.shape[0] // (HALVES * CHUNK) * CHUNK
    via = lax.ppermute(extra[cut:], 'fsdp', [(last, last ^ (n_dev // HALVES))])
    return [extra if s == 0 else lax.ppermute(extra if s < last else extra[:cut], 'fsdp', [(s, 0)]) for s in range(n_dev)], via


def join(extras, rest):
    return extras[:-1] + [(extras[-1], rest)]


def base_beside(base):
    return lax.all_to_all(base, 'fsdp', 0, 0, tiled=True)


def weight_body(n_rhs, steps, lhs_a_ref, lhs_b_ref, *refs):
    rhs_refs, (out_ref, turned_ref, rhs_ref, sems) = refs[:n_rhs], refs[n_rhs:]
    i = step_id()
    half = lhs_a_ref.shape[0]
    width = rhs_ref.shape[1]
    rows = rhs_ref.shape[0] // n_rhs

    def fill(j, n):
        cols = pl.ds(pl.multiple_of(j * steps, steps), n)
        return [pltpu.make_async_copy(v.at[:, cols], rhs_ref.at[pl.ds(k * rows, rows), cols], sems.at[k, j]) for k, v in enumerate(rhs_refs)]

    pieces = [(j, min(steps, width - j * steps)) for j in range(-(-width // steps))]

    @pl.when(i == 0)
    def _():
        for j, n in pieces:
            for copy in fill(j, n):
                copy.start()

    turned_ref[:, :half] = lhs_a_ref[:].T
    turned_ref[:, half:] = lhs_b_ref[:].T

    def product(at, n):
        out_ref[:, pl.ds(at, n)] = jnp.dot(turned_ref[:], rhs_ref[:, pl.ds(at, n)], preferred_element_type=F32)

    whole = width // steps

    @pl.loop(0, whole)
    def _(j):
        @pl.when(i == 0)
        def _():
            for copy in fill(j, steps):
                copy.wait()

        product(pl.multiple_of(j * steps, steps), steps)

    for j, n in pieces[whole:]:
        @pl.when(i == 0)
        def _():
            for copy in fill(j, n):
                copy.wait()

        product(j * steps, n)


def weight_grad(lhs_a, lhs_b, *rhs, more=0):
    half, height = lhs_a.shape
    width = rhs[0].shape[1]
    steps = 512
    blk = min(512, height)
    left = pl.BlockSpec((half, blk), lambda i: (0, i))
    return pl.pallas_call(
        functools.partial(weight_body, len(rhs), steps), grid=(height // blk,), in_specs=[left, left] + [HBM] * len(rhs), out_specs=row_spec(blk, width),
        out_shape=struct((height, width + more), F32),
        scratch_shapes=[pltpu.VMEM((blk, HALVES * half), BF16), pltpu.VMEM((HALVES * half, width), BF16), pltpu.SemaphoreType.DMA((len(rhs), -(-width // steps)))],
        compiler_params=params(FULL), name="weight_grad", cost_estimate=cost(lhs_a.size * width, lhs_a.size),
    )(lhs_a, lhs_b, *rhs)


def cut_body(order_ref, lhs_a_ref, lhs_b_ref, tail_ref, rhs_a_ref, rhs_b_ref, far_ref, near_ref, turned_ref, rhs_ref, sems):
    i = step_id()
    half = lhs_a_ref.shape[0]
    width = rhs_ref.shape[1]
    steps = 512
    whole = width // steps

    def fill(j, n, act):
        cols = pl.ds(pl.multiple_of(j * steps, steps), n)
        for k, v in enumerate((rhs_a_ref, rhs_b_ref)):
            getattr(pltpu.make_async_copy(v.at[:, cols], rhs_ref.at[pl.ds(k * half, half), cols], sems.at[k, j]), act)()

    @pl.when(i == 0)
    def _():
        @pl.loop(0, whole)
        def _(j):
            fill(j, steps, 'start')

        fill(whole, width - whole * steps, 'start')

    turned_ref[:, :half] = lhs_a_ref[:].T
    turned_ref[:, half:] = lhs_b_ref[:].T

    def product(j, n, out_ref):
        @pl.when(i == 0)
        def _():
            fill(j, n, 'wait')

        cols = pl.ds(pl.multiple_of(j * steps, steps), n)
        out_ref[:, cols] = jnp.dot(turned_ref[:], rhs_ref[:, cols], preferred_element_type=F32)

    far = i < pl.num_programs(0) // HALVES
    for mine, out_ref in ((far, far_ref), (~far, near_ref)):
        @pl.when(mine)
        def _():
            @pl.loop(0, whole)
            def _(j):
                product(j, steps, out_ref)

            product(whole, width - whole * steps, out_ref)
            out_ref[:, lane(width // LANES - 1)] += tail_ref[:]


def weight_grad_cut(lhs_a, lhs_b, tail, rhs_a, rhs_b, order):
    half, height = lhs_a.shape
    width = rhs_a.shape[1]
    n = order.shape[0]
    blk = height // n
    left = pl.BlockSpec((half, blk), lambda i, o: (0, o[i]))
    return pl.pallas_call(
        cut_body,
        grid_spec=pltpu.PrefetchScalarGridSpec(
            num_scalar_prefetch=1, grid=(n,), in_specs=[left, left, pl.BlockSpec((blk, LANES), lambda i, o: (o[i], 0)), HBM, HBM],
            out_specs=[pl.BlockSpec((blk, width), lambda i, o: (jnp.minimum(i, n // HALVES - 1), 0)),
                       pl.BlockSpec((blk, width), lambda i, o: (jnp.maximum(i - n // HALVES, 0), 0))],
            scratch_shapes=[pltpu.VMEM((blk, HALVES * half), BF16), pltpu.VMEM((HALVES * half, width), BF16), pltpu.SemaphoreType.DMA((HALVES, width // 512 + 1))]),
        out_shape=[struct((height // HALVES, width), F32)] * HALVES,
        compiler_params=params(FULL), name="weight_grad_cut", cost_estimate=cost(lhs_a.size * width, lhs_a.size),
    )(order, lhs_a, lhs_b, tail, rhs_a, rhs_b)


def sum_in_steps(far, near, n_dev, beside, hold):
    swap = lambda v, k: lax.ppermute(v, 'fsdp', [(i, i ^ k) for i in range(n_dev)])
    core, x, y = 1, 2, 4
    blocks = lambda v: v.reshape(n_dev // HALVES, -1, v.shape[1])
    at = far.shape[1] // PAIR * LANES
    other = swap(far, core)
    other, = beside(other)
    total = blocks(near) + blocks(other)
    left, right = hold(total[1::2, :, :at], total[2:, :, at:])
    left, right = swap(left, x), swap(right, y)
    keep_left, keep_right = total[::2, :, :at], total[:2, :, at:]
    left, right, keep_left, keep_right = beside(left, right, keep_left, keep_right)
    left, right = keep_left + left, keep_right + right
    last_left, last_right = swap(left[1], y), swap(right[1], x)
    return jnp.concatenate([left[0] + last_left, right[0] + last_right], axis=1)


def beside_body(lhs_a_ref, lhs_b_ref, rhs_a_ref, rhs_b_ref, _, out_ref, turned_ref):
    half = lhs_a_ref.shape[0]

    @pl.when(step_id() == 0)
    def _():
        turned_ref[:, :half] = lhs_a_ref[:].T
        turned_ref[:, half:] = lhs_b_ref[:].T

    prod = jnp.dot(turned_ref[:, :half], rhs_a_ref[:], preferred_element_type=F32)
    prod = prod + jnp.dot(turned_ref[:, half:], rhs_b_ref[:], preferred_element_type=F32)
    out_ref[:] = prod.reshape(out_ref.shape)


def weight_grad_beside(big, at, lhs_a, lhs_b, rhs_a, rhs_b, n_dev):
    half, height = lhs_a.shape
    rows, width = big.shape
    part = width - at
    parts = rhs_a.shape[1] // part
    big = big.reshape(n_dev, rows // n_dev, width)
    right = pl.BlockSpec((half, part), lambda q: (0, q))
    return pl.pallas_call(
        beside_body, grid=(parts,), in_specs=[whole_spec(lhs_a.shape)] * 2 + [right, right, HBM],
        out_specs=pl.BlockSpec((n_dev, height // n_dev, part), lambda q: (0, q, at // part)), out_shape=struct(big.shape, F32),
        scratch_shapes=[pltpu.VMEM((height, HALVES * half), BF16)], input_output_aliases={4: 0}, compiler_params=params(LARGE), name="weight_grad_beside",
        cost_estimate=cost(lhs_a.size * rhs_a.shape[1], lhs_a.size),
    )(lhs_a, lhs_b, rhs_a, rhs_b, big).reshape(rows, width)


def move_body(count_ref, from_ref, to_ref, x_ref, out_ref, sems):
    depth = sems.shape[0]

    @pl.loop(0, count_ref.shape[0])
    def _(o):
        n = count_ref[o]

        def copy(i):
            return pltpu.make_async_copy(x_ref.at[pl.ds(from_ref[o] + i, 1)], out_ref.at[pl.ds(to_ref[o] + i, 1)], sems.at[lax.rem(i, depth)])

        @pl.loop(0, n)
        def _(i):
            @pl.when(i >= depth)
            def _():
                copy(i - depth).wait()

            copy(i).start()

        @pl.loop(jnp.maximum(n - depth, 0), n)
        def _(i):
            copy(i).wait()


def move_rows(x, count, start_from, start_to, n_out):
    return pl.pallas_call(
        move_body, out_shape=struct((n_out,) + x.shape[1:], x.dtype),
        in_specs=[SCALARS] * 3 + [HBM], out_specs=HBM, scratch_shapes=[pltpu.SemaphoreType.DMA((16,))],
        name="move_rows")(count, start_from, start_to, x)


def rms_scale(in_vals, gain_vec):
    vals_f32 = in_vals.astype(F32)
    inv_rms = lax.rsqrt(jnp.mean(vals_f32 * vals_f32, axis=-1, keepdims=True) + RMS_EPS)
    return (vals_f32 * inv_rms * gain_vec).astype(BF16)


def dot(a, b, dims):
    return lax.dot_general(a, b, dims, preferred_element_type=F32)


NN = (((1,), (0,)), ((), ()))


def pack_body(o_ref, q_ref, down_ref, tail_ref, out_ref):
    low = low_lanes()
    start, width = o_ref.shape[1] // LANES, q_ref.shape[1] // LANES
    out_ref[:, lane(0, start)] = o_ref[:]
    for j in range(0, width, 3):
        one, two, three = (q_ref[:, lane(j + k)].astype(F32) for k in range(3))
        out_ref[:, lane(start + j)] = one.astype(BF16)
        out_ref[:, lane(start + j + 1)] = jnp.where(low, rotate(two, ROPE_DIM), rotate(three, ROPE_DIM)).astype(BF16)
        out_ref[:, lane(start + j + 2)] = jnp.where(low, two, three).astype(BF16)
    out_ref[:, lane(start + width, down_ref.shape[1] // LANES)] = down_ref[:]
    out_ref[:, lane(out_ref.shape[1] // LANES - 1)] = tail_ref[:]


def pack_weights(w_out, w_query, w_kv_down, gains):
    rows, width = w_query.shape
    cut = w_kv_down.shape[1] // LANES * LANES
    tail = jnp.concatenate([w_kv_down[:, cut:]] + [jnp.pad(g, (0, rows - g.shape[0]))[:, None] for g in gains], axis=1)
    tail = jnp.pad(tail, ((0, 0), (0, LANES - tail.shape[1])))
    return pl.pallas_call(pack_body, out_shape=struct((rows, w_out.shape[1] + width + cut + LANES), BF16),
                          name="pack_weights")(w_out, w_query, w_kv_down[:, :cut], tail)


def unpack_body(g_ref, q_ref, down_ref):
    low = low_lanes()
    width = q_ref.shape[1] // LANES
    for j in range(0, width, 3):
        plain, rot = rotate(g_ref[:, lane(j + 1)], ROPE_DIM), g_ref[:, lane(j + 2)]
        q_ref[:, lane(j)] = g_ref[:, lane(j)]
        q_ref[:, lane(j + 1)] = jnp.where(low, rot, plain)
        q_ref[:, lane(j + 2)] = jnp.where(low, plain, rot)
    down_ref[:] = g_ref[:, q_ref.shape[1]:q_ref.shape[1] + down_ref.shape[1]]


def unpack_grads(g_x, q_width, down_width):
    rows = g_x.shape[0]
    return pl.pallas_call(unpack_body, out_shape=[struct((rows, q_width), F32), struct((rows, down_width), F32)], name="unpack_grads")(g_x)


def share_body(n_dev, x_ref, out_ref, send_sems, recv_sems):
    place = lax.axis_index('fsdp')
    for m in range(n_dev):
        @pl.when(place == m)
        def _():
            copies = [pltpu.make_async_remote_copy(x_ref, out_ref.at[m], send_sems.at[d], recv_sems.at[m], device_id={'fsdp': d}, device_id_type=pl.DeviceIdType.MESH)
                      for d in range(n_dev) if d != m]
            for copy in copies:
                copy.start()
            out_ref[m] = x_ref[:]
            for copy in copies:
                copy.wait_send()
            for s in range(n_dev):
                if s != m:
                    pltpu.make_async_remote_copy(x_ref, out_ref.at[s], send_sems.at[s], recv_sems.at[s], device_id={'fsdp': s}, device_id_type=pl.DeviceIdType.MESH).wait_recv()


def share(x, n_dev):
    vmem = pl.BlockSpec(memory_space=pltpu.VMEM)
    wide = pltpu.SemaphoreType.DMA((n_dev,))
    return pl.pallas_call(functools.partial(share_body, n_dev), out_shape=struct((n_dev,) + x.shape, x.dtype), in_specs=[vmem], out_specs=vmem,
                          scratch_shapes=[wide, wide], compiler_params=pltpu.CompilerParams(has_side_effects=True), name="share")(x)


def solution(mesh):
    n_dev = mesh.shape['fsdp']
    tok_spec = P(('dp', 'fsdp'), None)
    seq_spec = P(('dp', 'fsdp'), None, None)
    part_vec = P(('dp', 'fsdp'))
    vec_spec = P('fsdp')
    mat_spec = P('fsdp', None)

    def step(tok_ids, grad_out, emb_table, norm_gain, w_query, w_kv_down, kv_gain, w_kv_up, w_out):
        seq_count, seq_len = tok_ids.shape
        vocab_dev, d_model = emb_table.shape
        tok = seq_count * seq_len
        half = tok // HALVES
        per_half = seq_count // HALVES
        me = lax.axis_index('fsdp')
        gather = lambda piece: lax.all_gather(piece, 'fsdp', tiled=True)
        scatter = lambda full: lax.psum_scatter(full, 'fsdp', scatter_dimension=0, tiled=True)
        tie = lax.optimization_barrier
        rows_dev, q_width = w_query.shape
        rank_dev, = kv_gain.shape
        kv_rank = rank_dev * n_dev
        pe_at = q_width + kv_rank
        pad_at = pe_at + ROPE_DIM
        dy = grad_out.reshape(tok, d_model)
        w_ox = gather(pack_weights(w_out, w_query, w_kv_down, (norm_gain, kv_gain)))

        base, extra = [-(-round(half * share) // CHUNK) * CHUNK for share in (0.09, 0.31)]
        n_slots = n_dev * base + extra
        uniq, rank = unique_rows(tok_ids.reshape(HALVES, half))
        all_uniq = share(uniq.reshape(-1, LANES), n_dev).reshape(n_dev, HALVES, half)
        below = lambda lists, edges: jnp.sum(lists[..., None, :] < edges[:, None], axis=-1, dtype=jnp.int32)
        starts = below(all_uniq, jnp.arange(n_dev + 1, dtype=jnp.int32) * vocab_dev)
        counts = starts[..., 1:] - starts[..., :-1]
        fits = jnp.all(counts <= jnp.asarray([base + extra] + [base] * (n_dev - 1), jnp.int32))
        lists = jnp.swapaxes(all_uniq, 0, 1).reshape(HALVES * n_dev, half) - me * vocab_dev
        edges = below(lists, jnp.arange(vocab_dev // TABLE_BLOCK + 1, dtype=jnp.int32) * TABLE_BLOCK)
        my_starts, named = (lax.dynamic_index_in_dim(v, me, keepdims=False) for v in (starts[..., :-1], counts))
        place = jnp.arange(half, dtype=jnp.int32)
        begun = place[:, None] >= my_starts[:, None, 1:]
        slot = place + jnp.sum(jnp.where(begun, base - named[:, None, :-1], 0), axis=-1)
        slot = jnp.where((place >= base) & ~begun[..., 0], place + (n_dev - 1) * base, slot)
        slot = jnp.where(fits, slot, place)
        slots = jnp.arange(n_dev, dtype=jnp.int32) * half
        (rank_a, rank_b), (slot_a, slot_b) = rank, slot

        base_a, base_b, *extras = pick_rows(emb_table, lists, edges, n_dev, base, extra)
        extras_a, extras_b = extras[:n_dev], extras[n_dev:]

        def fetch_any(h):
            mine = slice(h * n_dev, (h + 1) * n_dev)
            far, = pick_rows(emb_table, lists[mine], edges[mine], n_dev, half, 0)
            far, prod = exchange(far, [], n_dev, dy, w_ox)
            return move_rows(far, named[h], slots, my_starts[h], n_slots), prod

        recv, d_mix = lax.cond(fits, lambda: tuple(exchange(base_a, extras_a, n_dev, dy, w_ox)), lambda: fetch_any(0))
        recv, w_ox, w_kv_up, base_b, extras_b = tie((recv, w_ox, w_kv_up, base_b, extras_b))
        w_o, w_x = w_ox[:, :d_model], w_ox[:, d_model:]
        w_up = gather(w_kv_up)
        pieces = fetch_beside(base_b, extras_b)
        gain_vec = w_x[:, pad_at].astype(F32)
        kv_gain_vec = w_x[:, pad_at + 1].reshape(n_dev, rows_dev)[:, :rank_dev].reshape(kv_rank).astype(F32)

        def compute(h, x):
            qx = dot(x, w_x, NN).astype(BF16)
            latent = rms_scale(qx[:, q_width:pe_at], kv_gain_vec)
            kv = dot(latent, w_up, NN).astype(BF16)
            return (qx, latent) + tuple(attend(qx, kv, d_mix, h * per_half, per_half, pe_at // LANES))

        def descend(qx, d_qx, d_kv, d_pe):
            d_latent = dot(d_kv, w_up, COL_DIMS).astype(BF16)
            return latent_back(d_latent, qx, d_pe, kv_gain_vec, d_qx, q_width)

        h0_a, x_a = spread_rows([(recv, 0, None)], rank_a, slot_a, gain_vec, n_slots)
        qx_a, latent_a, mix_a, d_qx_a, d_kv_a, d_pe_a = compute(0, x_a)
        d_qx_a, kv_gain_a = descend(qx_a, d_qx_a, d_kv_a, d_pe_a)
        d_x = dot(d_qx_a, w_x, COL_DIMS).astype(BF16)
        *merged_a, gain_a = merge_rows(d_x, h0_a, dy, 0, gain_vec, rank_a, slot_a, n_dev * base, extra)
        (extra_a, via), got_a = bring_beside(merged_a[1], n_dev), base_beside(merged_a[0])

        pieces, gain_a = tie((pieces, gain_a))
        h0_b, x_b = lax.cond(
            fits, lambda v: spread_rows([(v[0], 0, None)] + [(p, n_dev * base, d) for d, p in enumerate(v[1:])], rank_b, slot_b, gain_vec, n_slots),
            lambda v: spread_rows([(fetch_any(1)[0], 0, None)], rank_b, slot_b, gain_vec, n_slots), pieces)
        qx_b, latent_b, mix_b, d_qx_b, d_kv_b, d_pe_b = compute(1, x_b)
        via, d_kv_b = tie((via, d_kv_b))
        extra_a = join(extra_a, lax.ppermute(via, 'fsdp', [(n_dev // HALVES - 1, 0)]))
        d_qx_b, kv_gain_b = descend(qx_b, d_qx_b, d_kv_b, d_pe_b)
        d_x = dot(d_qx_b, w_x, COL_DIMS).astype(BF16)
        *merged_b, gain_b = merge_rows(d_x, h0_b, dy, half, gain_vec, rank_b, slot_b, n_dev * base, extra)
        extra_b, via = bring_beside(merged_b[1], n_dev)

        mix_a, gain_b = tie((mix_a, gain_b))
        d_w_o = weight_grad(mix_a, mix_b, dy, more=w_up.size // d_model)
        d_w_o = weight_grad_beside(d_w_o, d_model, latent_a, latent_b, d_kv_a, d_kv_b, n_dev)
        g_o = scatter(d_w_o)
        x_a, d_w_o, merged_b[0], got_a, via = tie((x_a, d_w_o, merged_b[0], got_a, via))
        extra_b = join(extra_b, lax.ppermute(via, 'fsdp', [(n_dev // HALVES - 1, 0)]))
        got_b = base_beside(merged_b[0])
        kv_rows = jnp.pad((kv_gain_a + kv_gain_b).reshape(n_dev, rank_dev), ((0, 0), (0, rows_dev - rank_dev)))
        tail = jnp.stack([(gain_a + gain_b).reshape(d_model), kv_rows.reshape(d_model)], axis=1)
        tail = jnp.pad(tail, ((0, 0), (ROPE_DIM, LANES - ROPE_DIM - HALVES)))
        steps = jnp.arange(n_dev, dtype=jnp.int32)
        order = me ^ (jnp.where(steps < n_dev // HALVES, HALVES * steps + 1, HALVES * steps - n_dev))
        far, near = weight_grad_cut(x_a, x_b, tail, d_qx_a, d_qx_b, order)

        def bring_any(h, merged):
            far = move_rows(jnp.concatenate(merged, axis=0), named[h], my_starts[h], slots, n_dev * half)
            return exchange(far, [], n_dev, dy, w_ox)[0]

        made, rows_b = [], [(got_b, extra_b)]

        def hold(left, right):
            left, right, rows_b[0] = tie((left, right, rows_b[0]))
            return left, right

        def beside(*values):
            if not made:
                h0, mix, *values = tie((h0_a, mix_a, far))[:2] + tuple(values)
                outs = [(h0.astype(F32) + dot(mix, w_o, NN)).astype(BF16), (h0_b.astype(F32) + dot(mix_b, w_o, NN)).astype(BF16)]
                *outs, values[0] = tie((*outs, values[0]))
                made.append(jnp.concatenate(outs, axis=0))
            else:
                values = list(values)
                edges_now, values[2] = tie((edges, values[2]))
                made.append(lax.cond(
                    fits, lambda: add_rows([(got_a, base, base, extra_a), (rows_b[0][0], base, base, rows_b[0][1])], lists, edges_now, n_dev, vocab_dev),
                    lambda: add_rows([(bring_any(h, v), half, half, []) for h, v in enumerate((merged_a, merged_b))], lists, edges_now, n_dev, vocab_dev)))
                made[1], values[0] = tie((made[1], values[0]))
            return values

        g_x = sum_in_steps(far, near, n_dev, beside, hold)
        out, grad_table = made
        g_up = jnp.swapaxes(g_o[:, d_model:].reshape(-1, rank_dev, g_o.shape[1] - d_model), 0, 1).reshape(w_kv_up.shape)
        g_query, g_down = unpack_grads(g_x, q_width, pad_at - q_width)
        return (out.reshape(seq_count, seq_len, d_model), grad_table, g_x[:, pad_at], g_query,
                g_down, g_x[:rank_dev, pad_at + 1], g_up, g_o[:, :d_model])

    return jax.shard_map(step, mesh=mesh, in_specs=(tok_spec, seq_spec, mat_spec, vec_spec, mat_spec, mat_spec, vec_spec, mat_spec, mat_spec), out_specs=(seq_spec, tok_spec, part_vec, tok_spec, tok_spec, part_vec, tok_spec, tok_spec), check_vma=False)
```

profile of v0, /device:TPU:0, one launch (start us, length us, event | category | flops | bytes accessed | tf_op | source)
XLA Modules:
  0.0 1335.6 jit_solution(12215996367546213813)
XLA Ops:
  48.9 63.3 %pick_rows.4 = (bf16[896,16,128]{2,1,0:T(8,128)(2,1)}, bf16[896,16,128]{2,1,0:T(8,128)(2,1)}, bf16[368,16,128]{2,1,0:T(8,128)(2,1)S(1)}, bf16[368,16,128]{2,1,0:...) custom-call(s32[18440]{0:T(1024)} %pad.35.rows_ref, ...), custom_call_target="tpu_custom_call" | custom-call | flops 60000000 | bytes 10000000 | tf_op jit(solution)/shard_map/pick_rows/pallas_call | solution.py:200
  112.2 22.7 %all-gather.3.cloned.1.call-done = bf16[2048,5760]{1,0:T(8,128)(2,1)} async-done(((bf16[256,5760]{1,0:T(8,128)(2,1)}), bf16[2048,5760]{1,0:T(8,128)(2,1)}) %all-gather.3.cloned.1.call-update) | async-done | bytes 23592976 | tf_op jit(solution)/shard_map/all_gather | solution.py:978
  134.9 86.0 %conditional.3 = (bf16[1264,16,128]{2,1,0:T(8,128)(2,1)}, bf16[2304,2048]{1,0:T(8,128)(2,1)}) conditional(s32[]{:T(128)} %convert_element_type.108, (s32[2,8]{1,0:T(2,128)S(1)}, s32[2,8]{1,0:T(2,128)S(1)}, s32[16,1152]{1,0:T(8,128)S(1)}, s32[16,21]{0,1:T(8,128)S(1)}, bf16[20480,2048]{1,0:T(8,128)(2,1)}, /*index=5*/bf16[2304,2048]{1,0:T(8,128)(2,1)}, ...), branch_computations={%region_5.6_spmd, %region_6.7_spmd} | conditional | flops 22265171279872 | bytes 14945488 | solution.py:1017
  134.9 86.0 %exchange.7 = (bf16[1264,16,128]{2,1,0:T(8,128)(2,1)}, bf16[4,368,16,128]{3,2,1,0:T(8,128)(2,1)}, bf16[2304,2048]{1,0:T(8,128)(2,1)}) custom-call(bf16[896,16,128]{2,1,0:T(8,128)(2,1)} %get-tuple-element.185.base_ref, bf16[368,16,128]{2,1,0:T(8,128)(2,1)S(1)} %get-tuple-element.186.refs_0_, bf16[368,16,128]{2,1,0:T(8,128)(2,1)} %get-tuple-element.187.refs_1_, ...), custom_call_target="tpu_custom_call" | custom-call | flops 22265110462464 | bytes 4718592 | tf_op jit(solution)/shard_map/cond/branch_1_fun/exchange/pallas_call | solution.py:664
  255.7 24.6 %convolution_convert_fusion.3.q_ref.pe_ref.c_ref = bf16[1152,3712]{1,0:T(8,128)(2,1)} fusion(bf16[1152,2048]{1,0:T(8,128)(2,1)S(1)} %get-tuple-element.436.lhs_a_ref, bf16[2048,5760]{1,0:T(8,128)(2,1)} %all-gather.3.cloned.1.call-done), kind=kOutput, calls=%fused_computation.17 | convolution fusion | flops 17519689728 | bytes 28475392 | tf_op jit(solution)/shard_map/dot_general | solution.py:895
  293.9 37.0 %attention.2 = (bf16[1152,2048]{1,0:T(8,128)(2,1)S(1)}, bf16[1152,3712]{1,0:T(8,128)(2,1)S(1)}, bf16[1152,4096]{1,0:T(8,128)(2,1)}, bf16[1152,128]{1,0:T(8,128)(2,1)S(1)}) custom-call(bf16[1152,3712]{1,0:T(8,128)(2,1)} %convolution_convert_fusion.3.q_ref.pe_ref.c_ref, bf16[1152,3712]{1,0:T(8,128)(2,1)} %convolution_convert_fusion.3.q_ref.pe_ref.c_ref, ...), custom_call_target="tpu_custom_call" | custom-call | flops 4926210048 | bytes 4276224 | tf_op jit(solution)/shard_map/attention/pallas_call | solution.py:346
  330.8 12.3 convolution_convert_fusion.5.w_ref
  358.0 23.8 %fusion.6.dx_ref = bf16[1152,2048]{1,0:T(8,128)(2,1)S(1)} fusion(bf16[1152,3712]{1,0:T(8,128)(2,1)} %get-tuple-element.402.rhs_a_ref, bf16[2048,5760]{1,0:T(8,128)(2,1)} %all-gather.3.cloned.1.call-done), kind=kOutput, calls=%fused_computation.27 | convolution fusion | flops 17517772800 | bytes 28475392 | tf_op jit(solution)/shard_map/dot_general | solution.py:895
  381.8 15.8 %merge_rows.2 = (f32[896,16,128]{2,1,0:T(8,128)}, f32[368,16,128]{2,1,0:T(8,128)}, f32[1,2048]{1,0:T(1,128)S(1)}) custom-call(s32[1152]{0:T(1024)S(1)} %get-tuple-element.682.rank_ref, s32[1152]{0:T(1024)S(1)} %get-tuple-element.662.slot_ref, bf16[1152,2048]{1,0:T(8,128)(2,1)S(1)} %fusion.6.dx_ref, bf16[1152,2048]{1,0:T(8,128)(2,1)S(1)} %bitcast.80, ...), custom_call_target="tpu_custom_call" | custom-call | flops 60000000 | bytes 10000000 | tf_op jit(solution)/shard_map/merge_rows/pallas_call | solution.py:461
  402.3 15.2 %conditional.4 = (bf16[1152,2048]{1,0:T(8,128)(2,1)}, bf16[1152,2048]{1,0:T(8,128)(2,1)S(1)}, f32[1152,2048]{1,0:T(8,128)S(1)}) conditional(s32[]{:T(128)} %convert_element_type.108, (f32[2048]{0:T(1024)S(1)}, s32[2,8]{1,0:T(2,128)S(1)}, s32[2,8]{1,0:T(2,128)S(1)}, s32[16,1152]{1,0:T(8,128)S(1)}, s32[16,21]{0,1:T(8,128)S(1)}, ...), branch_computations={%region_8.9_spmd.clone, %region_9.10_spmd.clone} | conditional | flops 22265234194432 | bytes 59810676 | solution.py:1043
  402.3 11.6 spread_rows.7
  421.2 23.7 %convolution_convert_fusion.2.q_ref.pe_ref.c_ref = bf16[1152,3712]{1,0:T(8,128)(2,1)S(1)} fusion(bf16[1152,2048]{1,0:T(8,128)(2,1)S(1)} %get-tuple-element.423.lhs_b_ref, bf16[2048,5760]{1,0:T(8,128)(2,1)} %all-gather.3.cloned.1.call-done), kind=kOutput, calls=%fused_computation.16 | convolution fusion | flops 17519689728 | bytes 28475392 | tf_op jit(solution)/shard_map/dot_general | solution.py:895
  454.2 37.1 %attention.3 = (bf16[1152,2048]{1,0:T(8,128)(2,1)S(1)}, bf16[1152,3712]{1,0:T(8,128)(2,1)S(1)}, bf16[1152,4096]{1,0:T(8,128)(2,1)}, bf16[1152,128]{1,0:T(8,128)(2,1)S(1)}) custom-call(bf16[1152,3712]{1,0:T(8,128)(2,1)} %copy-done.18, bf16[1152,3712]{1,0:T(8,128)(2,1)} %copy-done.18, bf16[1152,4096]{1,0:T(8,128)(2,1)} %convolution_convert_fusion.kv_ref, ...), custom_call_target="tpu_custom_call" | custom-call | flops 4926210048 | bytes 4276224 | tf_op jit(solution)/shard_map/attention/pallas_call | solution.py:346
  491.3 15.2 %convolution_convert_fusion.4.w_ref = bf16[1152,512]{1,0:T(8,128)(2,1)} fusion(bf16[1152,4096]{1,0:T(8,128)(2,1)} %get-tuple-element.425.rhs_b_ref, bf16[512,4096]{1,0:T(8,128)(2,1)} %all-gather.5.cloned.1.call-done), kind=kOutput, calls=%fused_computation.33 | convolution fusion | flops 4832428032 | bytes 14811136 | tf_op jit(solution)/shard_map/dot_general | solution.py:895
  511.0 23.9 %fusion.9.dx_ref = bf16[1152,2048]{1,0:T(8,128)(2,1)S(1)} fusion(bf16[1152,3712]{1,0:T(8,128)(2,1)} %get-tuple-element.428.rhs_b_ref, bf16[2048,5760]{1,0:T(8,128)(2,1)} %all-gather.3.cloned.1.call-done), kind=kOutput, calls=%fused_computation.28 | convolution fusion | flops 17517772800 | bytes 28475392 | tf_op jit(solution)/shard_map/dot_general | solution.py:895
  534.9 15.9 %merge_rows.3 = (f32[896,16,128]{2,1,0:T(8,128)}, f32[368,16,128]{2,1,0:T(8,128)}, f32[1,2048]{1,0:T(1,128)S(1)}) custom-call(s32[1152]{0:T(1024)S(1)} %get-tuple-element.681.rank_ref, s32[1152]{0:T(1024)S(1)} %get-tuple-element.661.slot_ref, bf16[1152,2048]{1,0:T(8,128)(2,1)S(1)} %fusion.9.dx_ref, bf16[1152,2048]{1,0:T(8,128)(2,1)} %get-tuple-element.429.h0_ref, ...), custom_call_target="tpu_custom_call" | custom-call | flops 60000000 | bytes 10000000 | tf_op jit(solution)/shard_map/merge_rows/pallas_call | solution.py:461
  550.9 29.9 %weight_grad.1 = f32[2048,3072]{1,0:T(8,128)} custom-call(bf16[1152,2048]{1,0:T(8,128)(2,1)} %copy-done.4, bf16[1152,2048]{1,0:T(8,128)(2,1)} %copy-done.5, bf16[2304,2048]{1,0:T(8,128)(2,1)} %bitcast.91), custom_call_target="tpu_custom_call" | custom-call | flops 4831838208 | bytes 2359296 | tf_op jit(solution)/shard_map/weight_grad/pallas_call | solution.py:744
  582.1 16.3 %weight_grad_beside.1 = f32[8,256,3072]{2,1,0:T(8,128)} custom-call(bf16[1152,512]{1,0:T(8,128)(2,1)S(1)} %copy-done.7, bf16[1152,512]{1,0:T(8,128)(2,1)S(1)} %copy-done.9, bf16[1152,4096]{1,0:T(8,128)(2,1)} %get-tuple-element.399.rhs_a_ref, bf16[1152,4096]{1,0:T(8,128)(2,1)} %get-tuple-element.425.rhs_b_ref, ...), custom_call_target="tpu_custom_call", output_to_operand_aliasing={{}: (4, {})} | custom-call | flops 2415919104 | bytes 589824 | tf_op jit(solution)/shard_map/weight_grad_beside/pallas_call | solution.py:850
  608.5 125.1 %all-to-all-done.1 = f32[896,16,128]{2,1,0:T(8,128)} async-done(((f32[896,16,128]{2,1,0:T(8,128)}), f32[896,16,128]{2,1,0:T(8,128)}, u32[]{:S(2)}, u32[]{:S(2)}) %all-to-all-start.1) | async-done | bytes 7340064 | tf_op jit(solution)/shard_map/all_to_all | solution.py:690
  733.6 57.4 %weight_grad_cut.1 = (f32[1024,3712]{1,0:T(8,128)}, f32[1024,3712]{1,0:T(8,128)}) custom-call(s32[8]{0:T(128)} %fusion.33.order_ref, bf16[1152,2048]{1,0:T(8,128)(2,1)} %copy-done.17, bf16[1152,2048]{1,0:T(8,128)(2,1)} %copy-done.51, f32[2048,128]{1,0:T(8,128)} %pad.37.tail_ref, bf16[1152,3712]{1,0:T(8,128)(2,1)} %get-tuple-element.402.rhs_a_ref, ...), custom_call_target="tpu_custom_call" | custom-call | flops 8757706752 | bytes 2359296 | tf_op jit(solution)/shard_map/weight_grad_cut/pallas_call | solution.py:801
  797.7 32.9 %all-to-all-start.2 = ((f32[896,16,128]{2,1,0:T(8,128)}), f32[896,16,128]{2,1,0:T(8,128)}, u32[]{:S(2)}, u32[]{:S(2)}) async-start(f32[896,16,128]{2,1,0:T(8,128)} %get-tuple-element.449), calls=%async_computation.2 | async-start | bytes 14680064 | tf_op jit(solution)/shard_map/all_to_all | solution.py:690
  830.6 31.1 %collective-permute-done.24 = f32[176,16,128]{2,1,0:T(8,128)S(1)} collective-permute-done((f32[176,16,128]{2,1,0:T(8,128)S(1)}, f32[176,16,128]{2,1,0:T(8,128)S(1)}, u32[]{:S(2)}, u32[]{:S(2)}) %collective-permute-start.24) | collective-permute-done | bytes 1441824 | tf_op jit(solution)/shard_map/ppermute | solution.py:682
  863.0 17.7 %collective-permute-done.23 = f32[368,16,128]{2,1,0:T(8,128)} collective-permute-done((f32[368,16,128]{2,1,0:T(8,128)}, f32[368,16,128]{2,1,0:T(8,128)}, u32[]{:S(2)}, u32[]{:S(2)}) %collective-permute-start.23) | collective-permute-done | bytes 3014688 | tf_op jit(solution)/shard_map/ppermute | solution.py:682
  882.0 77.6 %collective-permute-done.22 = f32[368,16,128]{2,1,0:T(8,128)} collective-permute-done((f32[368,16,128]{2,1,0:T(8,128)}, f32[368,16,128]{2,1,0:T(8,128)}, u32[]{:S(2)}, u32[]{:S(2)}) %collective-permute-start.22) | collective-permute-done | bytes 3014688 | tf_op jit(solution)/shard_map/ppermute | solution.py:682
  965.2 16.8 %add_convert_fusion = bf16[1152,2048]{1,0:T(8,128)(2,1)} fusion(f32[1152,2048]{1,0:T(8,128)} %copy-done.20, bf16[1152,2048]{1,0:T(8,128)(2,1)} %copy-done.5, bf16[2048,5760]{1,0:T(8,128)(2,1)} %all-gather.3.cloned.1.call-done), kind=kOutput, calls=%fused_computation.25 | convolution fusion | flops 9668395008 | bytes 27262976 | tf_op jit(solution)/shard_map/dot_general | solution.py:895
  998.1 13.9 %add_convert_fusion.1 = bf16[1152,2048]{1,0:T(8,128)(2,1)} fusion(bf16[1152,2048]{1,0:T(8,128)(2,1)S(1)} %bitcast.82, bf16[1152,2048]{1,0:T(8,128)(2,1)S(1)} %bitcast.84, bf16[2048,5760]{1,0:T(8,128)(2,1)} %all-gather.3.cloned.1.call-done), kind=kOutput, calls=%fused_computation.26 | convolution fusion | flops 9670754304 | bytes 22544384 | tf_op jit(solution)/shard_map/dot_general | solution.py:895
  1032.7 15.2 %all-to-all-done.2 = f32[896,16,128]{2,1,0:T(8,128)} async-done(((f32[896,16,128]{2,1,0:T(8,128)}), f32[896,16,128]{2,1,0:T(8,128)}, u32[]{:S(2)}, u32[]{:S(2)}) %all-to-all-start.2) | async-done | bytes 7340064 | tf_op jit(solution)/shard_map/all_to_all | solution.py:690
  1047.9 63.4 %collective-permute-done.14 = f32[368,16,128]{2,1,0:T(8,128)} collective-permute-done((f32[368,16,128]{2,1,0:T(8,128)}, f32[368,16,128]{2,1,0:T(8,128)}, u32[]{:S(2)}, u32[]{:S(2)}) %collective-permute-start.14) | collective-permute-done | bytes 3014688 | tf_op jit(solution)/shard_map/ppermute | solution.py:682
  1115.2 62.3 %collective-permute-done.11 = f32[368,16,128]{2,1,0:T(8,128)} collective-permute-done((f32[368,16,128]{2,1,0:T(8,128)}, f32[368,16,128]{2,1,0:T(8,128)}, u32[]{:S(2)}, u32[]{:S(2)}) %collective-permute-start.11) | collective-permute-done | bytes 3014688 | tf_op jit(solution)/shard_map/ppermute | solution.py:682
  1177.6 103.1 %conditional.5 = (bf16[20480,2048]{1,0:T(8,128)(2,1)}) conditional(s32[]{:T(128)} %convert_element_type.108, (s32[16,1152]{1,0:T(8,128)S(1)}, s32[16,21]{0,1:T(8,128)S(1)}, s32[2,8]{1,0:T(2,128)S(1)}, s32[2,8]{1,0:T(2,128)S(1)}, f32[896,16,128]{2,1,0:T(8,128)}, /*index=5*/f32[368,16,128]{2,1,0:T(8,128)}, s32[8]{0:T(128)S(1)}, ...), branch_computations={%region_11.12_spmd, %region_12.13_spmd} | conditional | flops 44530283839488 | bytes 61304420 | solution.py:1087
  1179.4 101.3 %add_rows.3 = bf16[20480,2048]{1,0:T(8,128)(2,1)} custom-call(s32[18440]{0:T(1024)} %pad.27.rows_ref, s32[176]{0:T(256)} %reshape.169.edge_ref, f32[896,16,128]{2,1,0:T(8,128)} %get-tuple-element.242.refs_0_, f32[368,16,128]{2,1,0:T(8,128)} %get-tuple-element.243.refs_1_, f32[368,16,128]{2,1,0:T(8,128)} %get-tuple-element.244.refs_2_, ...), custom_call_target="tpu_custom_call" | custom-call | flops 60000000 | bytes 10000000 | tf_op jit(solution)/shard_map/cond/branch_1_fun/add_rows/pallas_call | solution.py:572
  1294.6 13.1 collective-permute-done.29
  (302 shorter events, 230.1 us)
Async XLA Ops:
  9.4 125.5 %all-gather.3.cloned.1.call-start = ((), (), s32[]{:S(2)}) async-start(), calls=%async_computation.4 | async-start | bytes 26542080 | tf_op jit(solution)/shard_map/all_gather | solution.py:978
  18.3 265.3 %all-gather.5.cloned.1.call-start = ((), (), s32[]{:S(2)}) async-start(), calls=%async_computation.5 | async-start | bytes 4718592 | tf_op jit(solution)/shard_map/all_gather | solution.py:978
  224.4 173.3 %all-to-all-start = ((bf16[896,16,128]{2,1,0:T(8,128)(2,1)}), bf16[896,16,128]{2,1,0:T(8,128)(2,1)}, u32[]{:S(2)}, u32[]{:S(2)}) async-start(bf16[896,16,128]{2,1,0:T(8,128)(2,1)} %get-tuple-element.404), calls=%async_computation | async-start | bytes 7340032 | tf_op jit(solution)/shard_map/all_to_all | solution.py:690
  227.7 1095.9 %reduce-scatter.2.cloned.1.call-start = ((), (), s32[]{:S(2)}) async-start(), calls=%async_computation.6 | async-start | bytes 28311552 | tf_op jit(solution)/shard_map/reduce_scatter | solution.py:979
  227.7 119.8 %collective-permute-start.1 = (bf16[368,16,128]{2,1,0:T(8,128)(2,1)}, bf16[368,16,128]{2,1,0:T(8,128)(2,1)S(1)}, u32[]{:S(2)}, u32[]{:S(2)}) collective-permute-start(bf16[368,16,128]{2,1,0:T(8,128)(2,1)} %get-tuple-element.406), channel_id=1, source_target_pairs={{0,1}} | collective-permute-start | bytes 4521992 | tf_op jit(solution)/shard_map/ppermute | solution.py:674
  230.0 125.5 %collective-permute-start.2 = (bf16[368,16,128]{2,1,0:T(8,128)(2,1)}, bf16[368,16,128]{2,1,0:T(8,128)(2,1)}, u32[]{:S(2)}, u32[]{:S(2)}) collective-permute-start(bf16[368,16,128]{2,1,0:T(8,128)(2,1)} %get-tuple-element.407), channel_id=1, source_target_pairs={{0,2}} | collective-permute-start | bytes 4521992 | tf_op jit(solution)/shard_map/ppermute | solution.py:674
  233.9 163.8 %collective-permute-start.3 = (bf16[368,16,128]{2,1,0:T(8,128)(2,1)}, bf16[368,16,128]{2,1,0:T(8,128)(2,1)}, u32[]{:S(2)}, u32[]{:S(2)}) collective-permute-start(bf16[368,16,128]{2,1,0:T(8,128)(2,1)} %get-tuple-element.408), channel_id=1, source_target_pairs={{0,3}} | collective-permute-start | bytes 4521992 | tf_op jit(solution)/shard_map/ppermute | solution.py:674
  236.3 161.4 %collective-permute-start.4 = (bf16[368,16,128]{2,1,0:T(8,128)(2,1)}, bf16[368,16,128]{2,1,0:T(8,128)(2,1)}, u32[]{:S(2)}, u32[]{:S(2)}) collective-permute-start(bf16[368,16,128]{2,1,0:T(8,128)(2,1)} %get-tuple-element.409), channel_id=1, source_target_pairs={{0,4}} | collective-permute-start | bytes 4521992 | tf_op jit(solution)/shard_map/ppermute | solution.py:674
  238.8 158.9 %collective-permute-start.5 = (bf16[368,16,128]{2,1,0:T(8,128)(2,1)}, bf16[368,16,128]{2,1,0:T(8,128)(2,1)}, u32[]{:S(2)}, u32[]{:S(2)}) collective-permute-start(bf16[368,16,128]{2,1,0:T(8,128)(2,1)} %get-tuple-element.410), channel_id=1, source_target_pairs={{0,5}} | collective-permute-start | bytes 4521992 | tf_op jit(solution)/shard_map/ppermute | solution.py:674
  347.5 50.2 %collective-permute-start.6 = (bf16[368,16,128]{2,1,0:T(8,128)(2,1)}, bf16[368,16,128]{2,1,0:T(8,128)(2,1)}, u32[]{:S(2)}, u32[]{:S(2)}) collective-permute-start(bf16[368,16,128]{2,1,0:T(8,128)(2,1)} %get-tuple-element.411), channel_id=1, source_target_pairs={{0,6}} | collective-permute-start | bytes 4521992 | tf_op jit(solution)/shard_map/ppermute | solution.py:674
  355.5 42.2 %collective-permute-start.7 = (bf16[368,16,128]{2,1,0:T(8,128)(2,1)}, bf16[368,16,128]{2,1,0:T(8,128)(2,1)}, u32[]{:S(2)}, u32[]{:S(2)}) collective-permute-start(bf16[368,16,128]{2,1,0:T(8,128)(2,1)} %get-tuple-element.412), channel_id=1, source_target_pairs={{0,7}} | collective-permute-start | bytes 4521992 | tf_op jit(solution)/shard_map/ppermute | solution.py:674
  400.4 90.9 %collective-permute-start = (f32[192,16,128]{2,1,0:T(8,128)}, f32[192,16,128]{2,1,0:T(8,128)}, u32[]{:S(2)}, u32[]{:S(2)}) collective-permute-start(f32[192,16,128]{2,1,0:T(8,128)} %slice.153), channel_id=1, source_target_pairs={{7,3}} | collective-permute-start | bytes 4718600 | tf_op jit(solution)/shard_map/ppermute | solution.py:681
  598.5 135.1 %all-to-all-start.1 = ((f32[896,16,128]{2,1,0:T(8,128)}), f32[896,16,128]{2,1,0:T(8,128)}, u32[]{:S(2)}, u32[]{:S(2)}) async-start(f32[896,16,128]{2,1,0:T(8,128)} %get-tuple-element.434), calls=%async_computation.1 | async-start | bytes 14680064 | tf_op jit(solution)/shard_map/all_to_all | solution.py:690
  791.0 205.8 %collective-permute-start.9 = (f32[1024,3712]{1,0:T(8,128)}, f32[1024,3712]{1,0:T(8,128)}, u32[]{:S(2)}, u32[]{:S(2)}) collective-permute-start(f32[1024,3712]{1,0:T(8,128)} %get-tuple-element.441), channel_id=1, source_target_pairs={{0,1},{1,0},{2,3},{3,2},{4,5},{5,4},{6,7},{7,6}} | collective-permute-start | bytes 45613064 | tf_op jit(solution)/shard_map/ppermute | solution.py:814
  791.0 89.7 %collective-permute-start.23 = (f32[368,16,128]{2,1,0:T(8,128)}, f32[368,16,128]{2,1,0:T(8,128)}, u32[]{:S(2)}, u32[]{:S(2)}) collective-permute-start(f32[368,16,128]{2,1,0:T(8,128)} %get-tuple-element.454), channel_id=1, source_target_pairs={{6,0}} | collective-permute-start | bytes 9043976 | tf_op jit(solution)/shard_map/ppermute | solution.py:682
  792.3 167.3 %collective-permute-start.22 = (f32[368,16,128]{2,1,0:T(8,128)}, f32[368,16,128]{2,1,0:T(8,128)}, u32[]{:S(2)}, u32[]{:S(2)}) collective-permute-start(f32[368,16,128]{2,1,0:T(8,128)} %get-tuple-element.454), channel_id=1, source_target_pairs={{5,0}} | collective-permute-start | bytes 9043976 | tf_op jit(solution)/shard_map/ppermute | solution.py:682
  793.6 170.0 %collective-permute-start.21 = (f32[368,16,128]{2,1,0:T(8,128)}, f32[368,16,128]{2,1,0:T(8,128)}, u32[]{:S(2)}, u32[]{:S(2)}) collective-permute-start(f32[368,16,128]{2,1,0:T(8,128)} %get-tuple-element.454), channel_id=1, source_target_pairs={{4,0}} | collective-permute-start | bytes 9043976 | tf_op jit(solution)/shard_map/ppermute | solution.py:682
  796.4 65.3 %collective-permute-start.24 = (f32[176,16,128]{2,1,0:T(8,128)S(1)}, f32[176,16,128]{2,1,0:T(8,128)S(1)}, u32[]{:S(2)}, u32[]{:S(2)}) collective-permute-start(f32[176,16,128]{2,1,0:T(8,128)S(1)} %slice.161), channel_id=1, source_target_pairs={{7,0}} | collective-permute-start | bytes 4325384 | tf_op jit(solution)/shard_map/ppermute | solution.py:682
  797.7 250.2 %all-to-all-start.2 = ((f32[896,16,128]{2,1,0:T(8,128)}), f32[896,16,128]{2,1,0:T(8,128)}, u32[]{:S(2)}, u32[]{:S(2)}) async-start(f32[896,16,128]{2,1,0:T(8,128)} %get-tuple-element.449), calls=%async_computation.2 | async-start | bytes 14680064 | tf_op jit(solution)/shard_map/all_to_all | solution.py:690
  861.7 120.3 %collective-permute-start.20 = (f32[368,16,128]{2,1,0:T(8,128)}, f32[368,16,128]{2,1,0:T(8,128)S(1)}, u32[]{:S(2)}, u32[]{:S(2)}) collective-permute-start(f32[368,16,128]{2,1,0:T(8,128)} %get-tuple-element.454), channel_id=1, source_target_pairs={{3,0}} | collective-permute-start | bytes 9043976 | tf_op jit(solution)/shard_map/ppermute | solution.py:682
  880.7 102.6 %collective-permute-start.19 = (f32[368,16,128]{2,1,0:T(8,128)}, f32[368,16,128]{2,1,0:T(8,128)S(1)}, u32[]{:S(2)}, u32[]{:S(2)}) collective-permute-start(f32[368,16,128]{2,1,0:T(8,128)} %get-tuple-element.454), channel_id=1, source_target_pairs={{2,0}} | collective-permute-start | bytes 9043976 | tf_op jit(solution)/shard_map/ppermute | solution.py:682
  963.6 31.8 %collective-permute-start.25 = (f32[192,16,128]{2,1,0:T(8,128)}, f32[192,16,128]{2,1,0:T(8,128)}, u32[]{:S(2)}, u32[]{:S(2)}) collective-permute-start(f32[192,16,128]{2,1,0:T(8,128)} %collective-permute-done.8), channel_id=1, source_target_pairs={{3,0}} | collective-permute-start | bytes 4718600 | tf_op jit(solution)/shard_map/ppermute | solution.py:1059
  982.0 65.8 %collective-permute-start.15 = (f32[368,16,128]{2,1,0:T(8,128)}, f32[368,16,128]{2,1,0:T(8,128)}, u32[]{:S(2)}, u32[]{:S(2)}) collective-permute-start(f32[368,16,128]{2,1,0:T(8,128)} %get-tuple-element.403), channel_id=1, source_target_pairs={{6,0}} | collective-permute-start | bytes 9043976 | tf_op jit(solution)/shard_map/ppermute | solution.py:682
  983.4 127.9 %collective-permute-start.14 = (f32[368,16,128]{2,1,0:T(8,128)}, f32[368,16,128]{2,1,0:T(8,128)}, u32[]{:S(2)}, u32[]{:S(2)}) collective-permute-start(f32[368,16,128]{2,1,0:T(8,128)} %get-tuple-element.403), channel_id=1, source_target_pairs={{5,0}} | collective-permute-start | bytes 9043976 | tf_op jit(solution)/shard_map/ppermute | solution.py:682
  984.7 127.9 %collective-permute-start.13 = (f32[368,16,128]{2,1,0:T(8,128)}, f32[368,16,128]{2,1,0:T(8,128)}, u32[]{:S(2)}, u32[]{:S(2)}) collective-permute-start(f32[368,16,128]{2,1,0:T(8,128)} %get-tuple-element.403), channel_id=1, source_target_pairs={{4,0}} | collective-permute-start | bytes 9043976 | tf_op jit(solution)/shard_map/ppermute | solution.py:682
  995.5 118.4 %collective-permute-start.12 = (f32[368,16,128]{2,1,0:T(8,128)}, f32[368,16,128]{2,1,0:T(8,128)}, u32[]{:S(2)}, u32[]{:S(2)}) collective-permute-start(f32[368,16,128]{2,1,0:T(8,128)} %get-tuple-element.403), channel_id=1, source_target_pairs={{3,0}} | collective-permute-start | bytes 9043976 | tf_op jit(solution)/shard_map/ppermute | solution.py:682
  996.8 51.1 %collective-permute-start.16 = (f32[176,16,128]{2,1,0:T(8,128)}, f32[176,16,128]{2,1,0:T(8,128)}, u32[]{:S(2)}, u32[]{:S(2)}) collective-permute-start(f32[176,16,128]{2,1,0:T(8,128)} %slice.158), channel_id=1, source_target_pairs={{7,0}} | collective-permute-start | bytes 4325384 | tf_op jit(solution)/shard_map/ppermute | solution.py:682
  1047.9 232.9 %collective-permute-start.26 = (f32[2,256,1792]{2,1,0:T(8,128)}, f32[2,256,1792]{2,1,0:T(8,128)}, u32[]{:S(2)}, u32[]{:S(2)}) collective-permute-start(f32[2,256,1792]{2,1,0:T(8,128)} %get-tuple-element.463), channel_id=1, source_target_pairs={{0,2},{1,3},{2,0},{3,1},{4,6},{5,7},{6,4},{7,5}} | collective-permute-start | bytes 11010056 | tf_op jit(solution)/shard_map/ppermute | solution.py:814
  1047.9 236.7 %collective-permute-start.27 = (f32[2,256,1920]{2,1,0:T(8,128)}, f32[2,256,1920]{2,1,0:T(8,128)}, u32[]{:S(2)}, u32[]{:S(2)}) collective-permute-start(f32[2,256,1920]{2,1,0:T(8,128)} %slice.183), channel_id=1, source_target_pairs={{0,4},{1,5},{2,6},{3,7},{4,0},{5,1},{6,2},{7,3}} | collective-permute-start | bytes 11796488 | tf_op jit(solution)/shard_map/ppermute | solution.py:814
  1111.3 66.2 %collective-permute-start.11 = (f32[368,16,128]{2,1,0:T(8,128)}, f32[368,16,128]{2,1,0:T(8,128)}, u32[]{:S(2)}, u32[]{:S(2)}) collective-permute-start(f32[368,16,128]{2,1,0:T(8,128)} %get-tuple-element.403), channel_id=1, source_target_pairs={{2,0}} | collective-permute-start | bytes 9043976 | tf_op jit(solution)/shard_map/ppermute | solution.py:682
  1112.6 64.9 %collective-permute-start.10 = (f32[368,16,128]{2,1,0:T(8,128)}, f32[368,16,128]{2,1,0:T(8,128)}, u32[]{:S(2)}, u32[]{:S(2)}) collective-permute-start(f32[368,16,128]{2,1,0:T(8,128)} %get-tuple-element.403), channel_id=1, source_target_pairs={{1,0}} | collective-permute-start | bytes 9043976 | tf_op jit(solution)/shard_map/ppermute | solution.py:682
  1113.9 63.6 %collective-permute-start.17 = (f32[192,16,128]{2,1,0:T(8,128)}, f32[192,16,128]{2,1,0:T(8,128)}, u32[]{:S(2)}, u32[]{:S(2)}) collective-permute-start(f32[192,16,128]{2,1,0:T(8,128)} %collective-permute-done), channel_id=1, source_target_pairs={{3,0}} | collective-permute-start | bytes 4718600 | tf_op jit(solution)/shard_map/ppermute | solution.py:1048
  (67 other events, 2533.5 us)
Sparse Core Ops, SparseCore 0:
  11.8 5.4 sort.11.cloned.1.call-done
  (1 shorter events, 0.0 us)
Sparse Core Ops, SparseCore 1:
  18.4 116.4 all-gather.2
  221.0 57.7 all-gather.4
  598.6 222.2 reduce-scatter.1
where the time goes:
time: 1350 us; the launch traced here: 1340 us
  Pallas kernels  521 us (39%)
  waiting for transfers between devices  443 us (33%)
  matrix products  172 us (13%)
  starting transfers between devices  88.8 us (7%)
  local copies, waits for them, and re-layouts  51.7 us (4%)
  other arithmetic  40.8 us (3%)
  between operations  18 us (1%)
    ppermute x14, waiting for transfers between devices, bring_beside(): lax.ppermute(extra if s < last else extra[:cut], 'fsdp', [(s, 0)])  252 us
    dot_general x10, matrix products, dot(): return lax.dot_general(a, b, dims, preferred_element_type=F32)  172 us
    all_to_all x3, waiting for transfers between devices, base_beside(): return lax.all_to_all(base, 'fsdp', 0, 0, tiled=True)  140 us
    pallas_call x1, Pallas kernels, add_rows(): pl.pallas_call(functools.partial(add_body, n_dev, n_tok, [(stride, base,...  101 us
    pallas_call x1, Pallas kernels, exchange(): pl.pallas_call(functools.partial(exchange_body, base, len(extras), n_dev)...  86 us
    pallas_call x2, Pallas kernels, attend(): pl.pallas_call(attn_body, grid=(seq_count, pairs), in_specs=[at(3 * LANES...  74.1 us
    pallas_call x1, Pallas kernels, pick_rows(): pl.pallas_call(functools.partial(pick_body, n_list, n_dev, n_tok, base, e...  63.3 us
    pallas_call x1, Pallas kernels, weight_grad_cut(): pl.pallas_call(cut_body, grid_spec=pltpu.PrefetchScalarGridSpec(num_scala...  57.4 us
  transfers between devices with their start and end apart: 36, of which 11 were waited for; matrix products, arithmetic and copies ran while one was open for 15% of the time, Pallas kernels for 27%

commit v1 on v0

--- a/solution.py
+++ b/solution.py
@@ -477,8 +477,8 @@
     sources = []
     for stride, base, extras in halves:
         first = flat.pop(0)
-        more = [[flat.pop(0) for _ in range(n)] for n in extras]
-        sources += [(first, d * stride, base, more[d] if extras else []) for d in range(n_dev)]
+        more = [flat.pop(0) for _ in range(extras)]
+        sources += [(first, d * stride, base, more[d] if extras else None) for d in range(n_dev)]
     b = step_id()
     n_blk = pl.num_programs(0)
     rows_blk, d_model = out_ref.shape
@@ -497,12 +497,10 @@
         def _():
             pltpu.make_async_copy(first.at[pl.ds(at + k * size, size)], dst, sem).start()
 
-        for ref in more:
-            @pl.when((k * size >= base) & (k * size < base + ref.shape[0]))
+        if more is not None:
+            @pl.when(k * size >= base)
             def _():
-                pltpu.make_async_copy(ref.at[pl.ds(k * size - base, size)], dst, sem).start()
-
-            base = base + ref.shape[0]
+                pltpu.make_async_copy(more.at[pl.ds(k * size - base, size)], dst, sem).start()
 
     def chunk_wait(s, k):
         dst, sem = landing(s, k)
@@ -565,12 +563,11 @@
     n_list, n_tok = rows.shape
     cols = halves[0][0].shape[1]
     d_model = cols * LANES
-    runs = [[v if isinstance(v, tuple) else (v,) for v in more] for *_, more in halves]
-    arrays = [v for half, more in zip(halves, runs) for v in [half[0]] + [u for run in more for u in run]]
+    arrays = [v for first, _, _, more in halves for v in [first] + more]
     block = HALVES * TABLE_BLOCK
     edges = edges[:, ::HALVES]
     return pl.pallas_call(
-        functools.partial(add_body, n_dev, n_tok, [(stride, base, [len(run) for run in more]) for (_, stride, base, _), more in zip(halves, runs)]),
+        functools.partial(add_body, n_dev, n_tok, [(stride, base, len(more)) for _, stride, base, more in halves]),
         grid_spec=pltpu.PrefetchScalarGridSpec(
             num_scalar_prefetch=2, grid=(n_rows // block,), in_specs=[HBM] * len(arrays), out_specs=row_spec(block, d_model),
             scratch_shapes=[pltpu.VMEM(((block + 1) * PITCH, LANES), F32),
@@ -669,21 +666,20 @@
     )(base_rows, *extras, lhs, rhs)[::HALVES]
 
 
+def between(src, dst, n_dev):
+    return [(src, dst), (dst, src)] + [(i, i) for i in range(n_dev) if i not in (src, dst)]
+
+
 def fetch_beside(base, extras):
     got = base_beside(base)
-    more = [v if d == 0 else lax.ppermute(v, 'fsdp', [(0, d)]) for d, v in enumerate(extras)]
+    more = [v if d == 0 else lax.ppermute(v, 'fsdp', between(0, d, len(extras))) for d, v in enumerate(extras)]
     return [got] + more
 
 
 def bring_beside(extra, n_dev):
     last = n_dev - 1
-    cut = extra.shape[0] // (HALVES * CHUNK) * CHUNK
-    via = lax.ppermute(extra[cut:], 'fsdp', [(last, last ^ (n_dev // HALVES))])
-    return [extra if s == 0 else lax.ppermute(extra if s < last else extra[:cut], 'fsdp', [(s, 0)]) for s in range(n_dev)], via
-
-
-def join(extras, rest):
-    return extras[:-1] + [(extras[-1], rest)]
+    via = lax.ppermute(extra, 'fsdp', [(last, last ^ (n_dev // HALVES))])
+    return [extra if s == 0 else lax.ppermute(extra, 'fsdp', [(s, 0)]) for s in range(last)], via
 
 
 def base_beside(base):
@@ -1045,7 +1041,7 @@
             lambda v: spread_rows([(fetch_any(1)[0], 0, None)], rank_b, slot_b, gain_vec, n_slots), pieces)
         qx_b, latent_b, mix_b, d_qx_b, d_kv_b, d_pe_b = compute(1, x_b)
         via, d_kv_b = tie((via, d_kv_b))
-        extra_a = join(extra_a, lax.ppermute(via, 'fsdp', [(n_dev // HALVES - 1, 0)]))
+        extra_a = extra_a + [lax.ppermute(via, 'fsdp', [(n_dev // 2 - 1, 0)])]
         d_qx_b, kv_gain_b = descend(qx_b, d_qx_b, d_kv_b, d_pe_b)
         d_x = dot(d_qx_b, w_x, COL_DIMS).astype(BF16)
         *merged_b, gain_b = merge_rows(d_x, h0_b, dy, half, gain_vec, rank_b, slot_b, n_dev * base, extra)
@@ -1055,8 +1051,7 @@
         d_w_o = weight_grad(mix_a, mix_b, dy, more=w_up.size // d_model)
         d_w_o = weight_grad_beside(d_w_o, d_model, latent_a, latent_b, d_kv_a, d_kv_b, n_dev)
         g_o = scatter(d_w_o)
-        x_a, d_w_o, merged_b[0], got_a, via = tie((x_a, d_w_o, merged_b[0], got_a, via))
-        extra_b = join(extra_b, lax.ppermute(via, 'fsdp', [(n_dev // HALVES - 1, 0)]))
+        x_a, d_w_o, merged_b[0], got_a = tie((x_a, d_w_o, merged_b[0], got_a))
         got_b = base_beside(merged_b[0])
         kv_rows = jnp.pad((kv_gain_a + kv_gain_b).reshape(n_dev, rank_dev), ((0, 0), (0, rows_dev - rank_dev)))
         tail = jnp.stack([(gain_a + gain_b).reshape(d_model), kv_rows.reshape(d_model)], axis=1)
@@ -1064,6 +1059,8 @@
         steps = jnp.arange(n_dev, dtype=jnp.int32)
         order = me ^ (jnp.where(steps < n_dev // HALVES, HALVES * steps + 1, HALVES * steps - n_dev))
         far, near = weight_grad_cut(x_a, x_b, tail, d_qx_a, d_qx_b, order)
+        via, far = tie((via, far))
+        extra_b = extra_b + [lax.ppermute(via, 'fsdp', [(n_dev // HALVES - 1, 0)])]
 
         def bring_any(h, merged):
             far = move_rows(jnp.concatenate(merged, axis=0), named[h], my_starts[h], slots, n_dev * half)

time: 1350 us -> 1390 us (1.030)
  starting transfers between devices: 88.8 us -> 116 us
  waiting for transfers between devices: 443 us -> 463 us
    ppermute x25 -> x23, starting transfers between devices: 48.5 us -> 93.9 us  [the longest x7 70.9 us: fetch_beside(): lax.ppermute(v, 'fsdp', between(0, d, len(extras)))]
    ppermute x25 -> x23, waiting for transfers between devices: 262 us -> 286 us  [the longest x12 285 us: bring_beside(): lax.ppermute(extra, 'fsdp', [(s, 0)])]
    all_to_all x3, starting transfers between devices: 40.1 us -> 21.9 us  [base_beside(): return lax.all_to_all(base, 'fsdp', 0, 0, tiled=True)]
  transfers between devices with their start and end apart: 36 -> 34, of which waited for: 11 -> 9; matrix products, arithmetic and copies ran while one was open for 15% -> 14% of each run, Pallas kernels for 27% -> 26%
where the time goes in v1:
time: 1390 us; the launch traced here: 1370 us
  Pallas kernels  518 us (37%)
  waiting for transfers between devices  463 us (33%)
  matrix products  172 us (12%)
  starting transfers between devices  116 us (8%)
  local copies, waits for them, and re-layouts  44.8 us (3%)
  other arithmetic  39.5 us (3%)
  between operations  18 us (1%)
    ppermute x12, waiting for transfers between devices, bring_beside(): lax.ppermute(extra, 'fsdp', [(s, 0)])  285 us
    dot_general x10, matrix products, dot(): return lax.dot_general(a, b, dims, preferred_element_type=F32)  172 us
    all_to_all x3, waiting for transfers between devices, base_beside(): return lax.all_to_all(base, 'fsdp', 0, 0, tiled=True)  137 us
    pallas_call x1, Pallas kernels, add_rows(): pl.pallas_call(functools.partial(add_body, n_dev, n_tok, [(stride, base,...  99 us
    pallas_call x1, Pallas kernels, exchange(): pl.pallas_call(functools.partial(exchange_body, base, len(extras), n_dev)...  86 us
    pallas_call x2, Pallas kernels, attend(): pl.pallas_call(attn_body, grid=(seq_count, pairs), in_specs=[at(3 * LANES...  74.1 us
    ppermute x7, starting transfers between devices, fetch_beside(): lax.ppermute(v, 'fsdp', between(0, d, len(extras)))  70.9 us
    pallas_call x1, Pallas kernels, pick_rows(): pl.pallas_call(functools.partial(pick_body, n_list, n_dev, n_tok, base, e...  63.2 us
  transfers between devices with their start and end apart: 34, of which 9 were waited for; matrix products, arithmetic and copies ran while one was open for 14% of the time, Pallas kernels for 26%

profile of v1, /device:TPU:0, one launch (start us, length us, event | category | flops | bytes accessed | tf_op | source)
XLA Modules:
  0.0 1372.3 jit_solution(6687497824668664889)
XLA Ops:
  49.0 63.2 %pick_rows.4 = (bf16[896,16,128]{2,1,0:T(8,128)(2,1)}, bf16[896,16,128]{2,1,0:T(8,128)(2,1)}, bf16[368,16,128]{2,1,0:T(8,128)(2,1)S(1)}, bf16[368,16,128]{2,1,0:...) custom-call(s32[18440]{0:T(1024)} %pad.35.rows_ref, ...), custom_call_target="tpu_custom_call" | custom-call | flops 60000000 | bytes 10000000 | tf_op jit(solution)/shard_map/pick_rows/pallas_call | solution.py:200
  112.2 22.7 %all-gather.3.cloned.1.call-done = bf16[2048,5760]{1,0:T(8,128)(2,1)} async-done(((bf16[256,5760]{1,0:T(8,128)(2,1)}), bf16[2048,5760]{1,0:T(8,128)(2,1)}) %all-gather.3.cloned.1.call-update) | async-done | bytes 23592976 | tf_op jit(solution)/shard_map/all_gather | solution.py:974
  134.9 86.0 %conditional.3 = (bf16[1264,16,128]{2,1,0:T(8,128)(2,1)}, bf16[2304,2048]{1,0:T(8,128)(2,1)}) conditional(s32[]{:T(128)} %convert_element_type.108, (s32[2,8]{1,0:T(2,128)S(1)}, s32[2,8]{1,0:T(2,128)S(1)}, s32[16,1152]{1,0:T(8,128)S(1)}, s32[16,21]{0,1:T(8,128)S(1)}, bf16[20480,2048]{1,0:T(8,128)(2,1)}, /*index=5*/bf16[2304,2048]{1,0:T(8,128)(2,1)}, ...), branch_computations={%region_5.6_spmd, %region_6.7_spmd} | conditional | flops 22265171279872 | bytes 14945488 | solution.py:1013
  134.9 86.0 %exchange.7 = (bf16[1264,16,128]{2,1,0:T(8,128)(2,1)}, bf16[4,368,16,128]{3,2,1,0:T(8,128)(2,1)}, bf16[2304,2048]{1,0:T(8,128)(2,1)}) custom-call(bf16[896,16,128]{2,1,0:T(8,128)(2,1)} %get-tuple-element.181.base_ref, bf16[368,16,128]{2,1,0:T(8,128)(2,1)S(1)} %get-tuple-element.182.refs_0_, bf16[368,16,128]{2,1,0:T(8,128)(2,1)} %get-tuple-element.183.refs_1_, ...), custom_call_target="tpu_custom_call" | custom-call | flops 22265110462464 | bytes 4718592 | tf_op jit(solution)/shard_map/cond/branch_1_fun/exchange/pallas_call | solution.py:661
  245.9 13.4 collective-permute-start.4
  286.0 23.1 %convolution_convert_fusion.3.q_ref.pe_ref.c_ref = bf16[1152,3712]{1,0:T(8,128)(2,1)S(1)} fusion(bf16[1152,2048]{1,0:T(8,128)(2,1)S(1)} %get-tuple-element.430.lhs_a_ref, bf16[2048,5760]{1,0:T(8,128)(2,1)} %all-gather.3.cloned.1.call-done), kind=kOutput, calls=%fused_computation.17 | convolution fusion | flops 17519689728 | bytes 28475392 | tf_op jit(solution)/shard_map/dot_general | solution.py:891
  324.5 36.9 %attention.2 = (bf16[1152,2048]{1,0:T(8,128)(2,1)S(1)}, bf16[1152,3712]{1,0:T(8,128)(2,1)S(1)}, bf16[1152,4096]{1,0:T(8,128)(2,1)}, bf16[1152,128]{1,0:T(8,128)(2,1)S(1)}) custom-call(bf16[1152,3712]{1,0:T(8,128)(2,1)} %copy-done.19, bf16[1152,3712]{1,0:T(8,128)(2,1)} %copy-done.19, bf16[1152,4096]{1,0:T(8,128)(2,1)} %convolution_convert_fusion.1.kv_ref, ...), custom_call_target="tpu_custom_call" | custom-call | flops 4926210048 | bytes 4276224 | tf_op jit(solution)/shard_map/attention/pallas_call | solution.py:346
  361.4 12.3 convolution_convert_fusion.5.w_ref
  378.2 14.2 %collective-permute-start.6 = (bf16[368,16,128]{2,1,0:T(8,128)(2,1)}, bf16[368,16,128]{2,1,0:T(8,128)(2,1)}, u32[]{:S(2)}, u32[]{:S(2)}) collective-permute-start(bf16[368,16,128]{2,1,0:T(8,128)(2,1)} %get-tuple-element.405), channel_id=1, source_target_pairs={{0,6},{6,0},{1,1},{2,2},{3,3},{4,4},{5,5},{7,7}} | collective-permute-start | bytes 4521992 | tf_op jit(solution)/shard_map/ppermute | solution.py:675
  392.4 13.1 collective-permute-start.7
  405.5 23.8 %fusion.6.dx_ref = bf16[1152,2048]{1,0:T(8,128)(2,1)S(1)} fusion(bf16[1152,3712]{1,0:T(8,128)(2,1)} %get-tuple-element.396.rhs_a_ref, bf16[2048,5760]{1,0:T(8,128)(2,1)} %all-gather.3.cloned.1.call-done), kind=kOutput, calls=%fused_computation.27 | convolution fusion | flops 17517772800 | bytes 28475392 | tf_op jit(solution)/shard_map/dot_general | solution.py:891
  429.4 15.8 %merge_rows.2 = (f32[896,16,128]{2,1,0:T(8,128)}, f32[368,16,128]{2,1,0:T(8,128)}, f32[1,2048]{1,0:T(1,128)S(1)}) custom-call(s32[1152]{0:T(1024)S(1)} %get-tuple-element.672.rank_ref, s32[1152]{0:T(1024)S(1)} %get-tuple-element.652.slot_ref, bf16[1152,2048]{1,0:T(8,128)(2,1)S(1)} %fusion.6.dx_ref, bf16[1152,2048]{1,0:T(8,128)(2,1)S(1)} %bitcast.80, ...), custom_call_target="tpu_custom_call" | custom-call | flops 60000000 | bytes 10000000 | tf_op jit(solution)/shard_map/merge_rows/pallas_call | solution.py:461
  447.5 15.2 %conditional.4 = (bf16[1152,2048]{1,0:T(8,128)(2,1)}, bf16[1152,2048]{1,0:T(8,128)(2,1)S(1)}, f32[1152,2048]{1,0:T(8,128)S(1)}) conditional(s32[]{:T(128)} %convert_element_type.108, (f32[2048]{0:T(1024)S(1)}, s32[2,8]{1,0:T(2,128)S(1)}, s32[2,8]{1,0:T(2,128)S(1)}, s32[16,1152]{1,0:T(8,128)S(1)}, s32[16,21]{0,1:T(8,128)S(1)}, ...), branch_computations={%region_8.9_spmd.clone, %region_9.10_spmd.clone} | conditional | flops 22265234194432 | bytes 59810676 | solution.py:1039
  466.5 23.7 %convolution_convert_fusion.2.q_ref.pe_ref.c_ref = bf16[1152,3712]{1,0:T(8,128)(2,1)S(1)} fusion(bf16[1152,2048]{1,0:T(8,128)(2,1)S(1)} %get-tuple-element.417.lhs_b_ref, bf16[2048,5760]{1,0:T(8,128)(2,1)} %all-gather.3.cloned.1.call-done), kind=kOutput, calls=%fused_computation.16 | convolution fusion | flops 17519689728 | bytes 28475392 | tf_op jit(solution)/shard_map/dot_general | solution.py:891
  499.5 37.2 %attention.3 = (bf16[1152,2048]{1,0:T(8,128)(2,1)S(1)}, bf16[1152,3712]{1,0:T(8,128)(2,1)S(1)}, bf16[1152,4096]{1,0:T(8,128)(2,1)}, bf16[1152,128]{1,0:T(8,128)(2,1)S(1)}) custom-call(bf16[1152,3712]{1,0:T(8,128)(2,1)} %copy-done.18, bf16[1152,3712]{1,0:T(8,128)(2,1)} %copy-done.18, bf16[1152,4096]{1,0:T(8,128)(2,1)} %convolution_convert_fusion.kv_ref, ...), custom_call_target="tpu_custom_call" | custom-call | flops 4926210048 | bytes 4276224 | tf_op jit(solution)/shard_map/attention/pallas_call | solution.py:346
  536.7 15.2 %convolution_convert_fusion.4.w_ref = bf16[1152,512]{1,0:T(8,128)(2,1)} fusion(bf16[1152,4096]{1,0:T(8,128)(2,1)} %get-tuple-element.419.rhs_b_ref, bf16[512,4096]{1,0:T(8,128)(2,1)} %all-gather.5.cloned.1.call-done), kind=kOutput, calls=%fused_computation.33 | convolution fusion | flops 4832428032 | bytes 14811136 | tf_op jit(solution)/shard_map/dot_general | solution.py:891
  556.3 23.9 %fusion.9.dx_ref = bf16[1152,2048]{1,0:T(8,128)(2,1)S(1)} fusion(bf16[1152,3712]{1,0:T(8,128)(2,1)} %get-tuple-element.422.rhs_b_ref, bf16[2048,5760]{1,0:T(8,128)(2,1)} %all-gather.3.cloned.1.call-done), kind=kOutput, calls=%fused_computation.28 | convolution fusion | flops 17517772800 | bytes 28475392 | tf_op jit(solution)/shard_map/dot_general | solution.py:891
  580.3 15.9 %merge_rows.3 = (f32[896,16,128]{2,1,0:T(8,128)}, f32[368,16,128]{2,1,0:T(8,128)}, f32[1,2048]{1,0:T(1,128)S(1)}) custom-call(s32[1152]{0:T(1024)S(1)} %get-tuple-element.671.rank_ref, s32[1152]{0:T(1024)S(1)} %get-tuple-element.651.slot_ref, bf16[1152,2048]{1,0:T(8,128)(2,1)S(1)} %fusion.9.dx_ref, bf16[1152,2048]{1,0:T(8,128)(2,1)} %get-tuple-element.423.h0_ref, ...), custom_call_target="tpu_custom_call" | custom-call | flops 60000000 | bytes 10000000 | tf_op jit(solution)/shard_map/merge_rows/pallas_call | solution.py:461
  596.2 29.9 %weight_grad.1 = f32[2048,3072]{1,0:T(8,128)} custom-call(bf16[1152,2048]{1,0:T(8,128)(2,1)} %copy-done.4, bf16[1152,2048]{1,0:T(8,128)(2,1)} %copy-done.5, bf16[2304,2048]{1,0:T(8,128)(2,1)} %bitcast.89), custom_call_target="tpu_custom_call" | custom-call | flops 4831838208 | bytes 2359296 | tf_op jit(solution)/shard_map/weight_grad/pallas_call | solution.py:740
  627.4 16.3 %weight_grad_beside.1 = f32[8,256,3072]{2,1,0:T(8,128)} custom-call(bf16[1152,512]{1,0:T(8,128)(2,1)S(1)} %copy-done.7, bf16[1152,512]{1,0:T(8,128)(2,1)S(1)} %copy-done.9, bf16[1152,4096]{1,0:T(8,128)(2,1)} %get-tuple-element.393.rhs_a_ref, bf16[1152,4096]{1,0:T(8,128)(2,1)} %get-tuple-element.419.rhs_b_ref, ...), custom_call_target="tpu_custom_call", output_to_operand_aliasing={{}: (4, {})} | custom-call | flops 2415919104 | bytes 589824 | tf_op jit(solution)/shard_map/weight_grad_beside/pallas_call | solution.py:846
  657.2 123.3 %all-to-all-done.1 = f32[896,16,128]{2,1,0:T(8,128)} async-done(((f32[896,16,128]{2,1,0:T(8,128)}), f32[896,16,128]{2,1,0:T(8,128)}, u32[]{:S(2)}, u32[]{:S(2)}) %all-to-all-start.1) | async-done | bytes 7340064 | tf_op jit(solution)/shard_map/all_to_all | solution.py:686
  780.5 57.1 %weight_grad_cut.1 = (f32[1024,3712]{1,0:T(8,128)}, f32[1024,3712]{1,0:T(8,128)}) custom-call(s32[8]{0:T(128)} %fusion.33.order_ref, bf16[1152,2048]{1,0:T(8,128)(2,1)} %copy-done.17, bf16[1152,2048]{1,0:T(8,128)(2,1)} %copy-done.50, f32[2048,128]{1,0:T(8,128)} %pad.37.tail_ref, bf16[1152,3712]{1,0:T(8,128)(2,1)} %get-tuple-element.396.rhs_a_ref, ...), custom_call_target="tpu_custom_call" | custom-call | flops 8757706752 | bytes 2359296 | tf_op jit(solution)/shard_map/weight_grad_cut/pallas_call | solution.py:797
  853.2 72.6 %collective-permute-done.22 = f32[368,16,128]{2,1,0:T(8,128)} collective-permute-done((f32[368,16,128]{2,1,0:T(8,128)}, f32[368,16,128]{2,1,0:T(8,128)}, u32[]{:S(2)}, u32[]{:S(2)}) %collective-permute-start.22) | collective-permute-done | bytes 3014688 | tf_op jit(solution)/shard_map/ppermute | solution.py:682
  927.0 71.7 %collective-permute-done.21 = f32[368,16,128]{2,1,0:T(8,128)} collective-permute-done((f32[368,16,128]{2,1,0:T(8,128)}, f32[368,16,128]{2,1,0:T(8,128)}, u32[]{:S(2)}, u32[]{:S(2)}) %collective-permute-start.21) | collective-permute-done | bytes 3014688 | tf_op jit(solution)/shard_map/ppermute | solution.py:682
  1001.4 16.8 %add_convert_fusion = bf16[1152,2048]{1,0:T(8,128)(2,1)} fusion(f32[1152,2048]{1,0:T(8,128)} %copy-done.21, bf16[1152,2048]{1,0:T(8,128)(2,1)} %copy-done.5, bf16[2048,5760]{1,0:T(8,128)(2,1)} %all-gather.3.cloned.1.call-done), kind=kOutput, calls=%fused_computation.25 | convolution fusion | flops 9668395008 | bytes 27262976 | tf_op jit(solution)/shard_map/dot_general | solution.py:891
  1023.5 15.2 %add_convert_fusion.1 = bf16[1152,2048]{1,0:T(8,128)(2,1)} fusion(bf16[1152,2048]{1,0:T(8,128)(2,1)S(1)} %bitcast.82, bf16[1152,2048]{1,0:T(8,128)(2,1)} %copy-done.4, bf16[2048,5760]{1,0:T(8,128)(2,1)} %all-gather.3.cloned.1.call-done), kind=kOutput, calls=%fused_computation.26 | convolution fusion | flops 9670754304 | bytes 22544384 | tf_op jit(solution)/shard_map/dot_general | solution.py:891
  1058.0 13.6 all-to-all-done.2
  1071.6 63.4 %collective-permute-done.14 = f32[368,16,128]{2,1,0:T(8,128)} collective-permute-done((f32[368,16,128]{2,1,0:T(8,128)}, f32[368,16,128]{2,1,0:T(8,128)}, u32[]{:S(2)}, u32[]{:S(2)}) %collective-permute-start.14) | collective-permute-done | bytes 3014688 | tf_op jit(solution)/shard_map/ppermute | solution.py:682
  1138.9 77.8 %collective-permute-done.11 = f32[368,16,128]{2,1,0:T(8,128)} collective-permute-done((f32[368,16,128]{2,1,0:T(8,128)}, f32[368,16,128]{2,1,0:T(8,128)}, u32[]{:S(2)}, u32[]{:S(2)}) %collective-permute-start.11) | collective-permute-done | bytes 3014688 | tf_op jit(solution)/shard_map/ppermute | solution.py:682
  1216.7 100.7 %conditional.5 = (bf16[20480,2048]{1,0:T(8,128)(2,1)}) conditional(s32[]{:T(128)} %convert_element_type.108, (s32[16,1152]{1,0:T(8,128)S(1)}, s32[16,21]{0,1:T(8,128)S(1)}, s32[2,8]{1,0:T(2,128)S(1)}, s32[2,8]{1,0:T(2,128)S(1)}, f32[896,16,128]{2,1,0:T(8,128)}, /*index=5*/f32[368,16,128]{2,1,0:T(8,128)}, s32[8]{0:T(128)S(1)}, ...), branch_computations={%region_11.12_spmd, %region_12.13_spmd} | conditional | flops 44530283839488 | bytes 61304420 | solution.py:1084
  1218.5 99.0 %add_rows.3 = bf16[20480,2048]{1,0:T(8,128)(2,1)} custom-call(s32[18440]{0:T(1024)} %pad.27.rows_ref, s32[176]{0:T(256)} %reshape.169.edge_ref, f32[896,16,128]{2,1,0:T(8,128)} %get-tuple-element.238.refs_0_, f32[368,16,128]{2,1,0:T(8,128)} %get-tuple-element.239.refs_1_, f32[368,16,128]{2,1,0:T(8,128)} %get-tuple-element.240.refs_2_, ...), custom_call_target="tpu_custom_call" | custom-call | flops 60000000 | bytes 10000000 | tf_op jit(solution)/shard_map/cond/branch_1_fun/add_rows/pallas_call | solution.py:569
  1331.4 13.1 collective-permute-done.27
  (287 shorter events, 243.7 us)
Async XLA Ops:
  9.4 125.5 %all-gather.3.cloned.1.call-start = ((), (), s32[]{:S(2)}) async-start(), calls=%async_computation.4 | async-start | bytes 26542080 | tf_op jit(solution)/shard_map/all_gather | solution.py:974
  18.3 295.9 %all-gather.5.cloned.1.call-start = ((), (), s32[]{:S(2)}) async-start(), calls=%async_computation.5 | async-start | bytes 4718592 | tf_op jit(solution)/shard_map/all_gather | solution.py:974
  224.4 220.8 %all-to-all-start = ((bf16[896,16,128]{2,1,0:T(8,128)(2,1)}), bf16[896,16,128]{2,1,0:T(8,128)(2,1)}, u32[]{:S(2)}, u32[]{:S(2)}) async-start(bf16[896,16,128]{2,1,0:T(8,128)(2,1)} %get-tuple-element.398), calls=%async_computation | async-start | bytes 7340032 | tf_op jit(solution)/shard_map/all_to_all | solution.py:686
  227.7 1132.6 %reduce-scatter.2.cloned.1.call-start = ((), (), s32[]{:S(2)}) async-start(), calls=%async_computation.6 | async-start | bytes 28311552 | tf_op jit(solution)/shard_map/reduce_scatter | solution.py:975
  227.7 150.4 %collective-permute-start.1 = (bf16[368,16,128]{2,1,0:T(8,128)(2,1)}, bf16[368,16,128]{2,1,0:T(8,128)(2,1)S(1)}, u32[]{:S(2)}, u32[]{:S(2)}) collective-permute-start(bf16[368,16,128]{2,1,0:T(8,128)(2,1)} %get-tuple-element.400), channel_id=1, source_target_pairs={{0,1},{1,0},{2,2},{3,3},{4,4},{5,5},{6,6},{7,7}} | collective-permute-start | bytes 4521992 | tf_op jit(solution)/shard_map/ppermute | solution.py:675
  229.9 162.4 %collective-permute-start.2 = (bf16[368,16,128]{2,1,0:T(8,128)(2,1)}, bf16[368,16,128]{2,1,0:T(8,128)(2,1)}, u32[]{:S(2)}, u32[]{:S(2)}) collective-permute-start(bf16[368,16,128]{2,1,0:T(8,128)(2,1)} %get-tuple-element.401), channel_id=1, source_target_pairs={{0,2},{2,0},{1,1},{3,3},{4,4},{5,5},{6,6},{7,7}} | collective-permute-start | bytes 4521992 | tf_op jit(solution)/shard_map/ppermute | solution.py:675
  234.1 211.1 %collective-permute-start.3 = (bf16[368,16,128]{2,1,0:T(8,128)(2,1)}, bf16[368,16,128]{2,1,0:T(8,128)(2,1)}, u32[]{:S(2)}, u32[]{:S(2)}) collective-permute-start(bf16[368,16,128]{2,1,0:T(8,128)(2,1)} %get-tuple-element.402), channel_id=1, source_target_pairs={{0,3},{3,0},{1,1},{2,2},{4,4},{5,5},{6,6},{7,7}} | collective-permute-start | bytes 4521992 | tf_op jit(solution)/shard_map/ppermute | solution.py:675
  245.9 199.3 %collective-permute-start.4 = (bf16[368,16,128]{2,1,0:T(8,128)(2,1)}, bf16[368,16,128]{2,1,0:T(8,128)(2,1)}, u32[]{:S(2)}, u32[]{:S(2)}) collective-permute-start(bf16[368,16,128]{2,1,0:T(8,128)(2,1)} %get-tuple-element.403), channel_id=1, source_target_pairs={{0,4},{4,0},{1,1},{2,2},{3,3},{5,5},{6,6},{7,7}} | collective-permute-start | bytes 4521992 | tf_op jit(solution)/shard_map/ppermute | solution.py:675
  259.4 185.8 %collective-permute-start.5 = (bf16[368,16,128]{2,1,0:T(8,128)(2,1)}, bf16[368,16,128]{2,1,0:T(8,128)(2,1)}, u32[]{:S(2)}, u32[]{:S(2)}) collective-permute-start(bf16[368,16,128]{2,1,0:T(8,128)(2,1)} %get-tuple-element.404), channel_id=1, source_target_pairs={{0,5},{5,0},{1,1},{2,2},{3,3},{4,4},{6,6},{7,7}} | collective-permute-start | bytes 4521992 | tf_op jit(solution)/shard_map/ppermute | solution.py:675
  378.2 67.1 %collective-permute-start.6 = (bf16[368,16,128]{2,1,0:T(8,128)(2,1)}, bf16[368,16,128]{2,1,0:T(8,128)(2,1)}, u32[]{:S(2)}, u32[]{:S(2)}) collective-permute-start(bf16[368,16,128]{2,1,0:T(8,128)(2,1)} %get-tuple-element.405), channel_id=1, source_target_pairs={{0,6},{6,0},{1,1},{2,2},{3,3},{4,4},{5,5},{7,7}} | collective-permute-start | bytes 4521992 | tf_op jit(solution)/shard_map/ppermute | solution.py:675
  392.4 52.9 %collective-permute-start.7 = (bf16[368,16,128]{2,1,0:T(8,128)(2,1)}, bf16[368,16,128]{2,1,0:T(8,128)(2,1)}, u32[]{:S(2)}, u32[]{:S(2)}) collective-permute-start(bf16[368,16,128]{2,1,0:T(8,128)(2,1)} %get-tuple-element.406), channel_id=1, source_target_pairs={{0,7},{7,0},{1,1},{2,2},{3,3},{4,4},{5,5},{6,6}} | collective-permute-start | bytes 4521992 | tf_op jit(solution)/shard_map/ppermute | solution.py:675
  445.3 91.4 %collective-permute-start = (f32[368,16,128]{2,1,0:T(8,128)}, f32[368,16,128]{2,1,0:T(8,128)}, u32[]{:S(2)}, u32[]{:S(2)}) collective-permute-start(f32[368,16,128]{2,1,0:T(8,128)} %get-tuple-element.397), channel_id=1, source_target_pairs={{7,3}} | collective-permute-start | bytes 9043976 | tf_op jit(solution)/shard_map/ppermute | solution.py:681
  643.7 136.7 %all-to-all-start.1 = ((f32[896,16,128]{2,1,0:T(8,128)}), f32[896,16,128]{2,1,0:T(8,128)}, u32[]{:S(2)}, u32[]{:S(2)}) async-start(f32[896,16,128]{2,1,0:T(8,128)} %get-tuple-element.429), calls=%async_computation.1 | async-start | bytes 14680064 | tf_op jit(solution)/shard_map/all_to_all | solution.py:686
  652.4 185.2 %collective-permute-start.8 = (f32[368,16,128]{2,1,0:T(8,128)}, f32[368,16,128]{2,1,0:T(8,128)}, u32[]{:S(2)}, u32[]{:S(2)}) collective-permute-start(f32[368,16,128]{2,1,0:T(8,128)} %get-tuple-element.449), channel_id=1, source_target_pairs={{7,3}} | collective-permute-start | bytes 9043976 | tf_op jit(solution)/shard_map/ppermute | solution.py:681
  837.6 184.5 %collective-permute-start.9 = (f32[1024,3712]{1,0:T(8,128)}, f32[1024,3712]{1,0:T(8,128)}, u32[]{:S(2)}, u32[]{:S(2)}) collective-permute-start(f32[1024,3712]{1,0:T(8,128)} %get-tuple-element.436), channel_id=1, source_target_pairs={{0,1},{1,0},{2,3},{3,2},{4,5},{5,4},{6,7},{7,6}} | collective-permute-start | bytes 45613064 | tf_op jit(solution)/shard_map/ppermute | solution.py:810
  837.8 88.0 %collective-permute-start.22 = (f32[368,16,128]{2,1,0:T(8,128)}, f32[368,16,128]{2,1,0:T(8,128)}, u32[]{:S(2)}, u32[]{:S(2)}) collective-permute-start(f32[368,16,128]{2,1,0:T(8,128)} %get-tuple-element.449), channel_id=1, source_target_pairs={{6,0}} | collective-permute-start | bytes 9043976 | tf_op jit(solution)/shard_map/ppermute | solution.py:682
  839.0 159.7 %collective-permute-start.21 = (f32[368,16,128]{2,1,0:T(8,128)}, f32[368,16,128]{2,1,0:T(8,128)}, u32[]{:S(2)}, u32[]{:S(2)}) collective-permute-start(f32[368,16,128]{2,1,0:T(8,128)} %get-tuple-element.449), channel_id=1, source_target_pairs={{5,0}} | collective-permute-start | bytes 9043976 | tf_op jit(solution)/shard_map/ppermute | solution.py:682
  840.3 159.7 %collective-permute-start.20 = (f32[368,16,128]{2,1,0:T(8,128)}, f32[368,16,128]{2,1,0:T(8,128)}, u32[]{:S(2)}, u32[]{:S(2)}) collective-permute-start(f32[368,16,128]{2,1,0:T(8,128)} %get-tuple-element.449), channel_id=1, source_target_pairs={{4,0}} | collective-permute-start | bytes 9043976 | tf_op jit(solution)/shard_map/ppermute | solution.py:682
  841.6 229.9 %all-to-all-start.2 = ((f32[896,16,128]{2,1,0:T(8,128)}), f32[896,16,128]{2,1,0:T(8,128)}, u32[]{:S(2)}, u32[]{:S(2)}) async-start(f32[896,16,128]{2,1,0:T(8,128)} %get-tuple-element.444), calls=%async_computation.2 | async-start | bytes 14680064 | tf_op jit(solution)/shard_map/all_to_all | solution.py:686
  851.6 166.6 %collective-permute-start.19 = (f32[368,16,128]{2,1,0:T(8,128)}, f32[368,16,128]{2,1,0:T(8,128)S(1)}, u32[]{:S(2)}, u32[]{:S(2)}) collective-permute-start(f32[368,16,128]{2,1,0:T(8,128)} %get-tuple-element.449), channel_id=1, source_target_pairs={{3,0}} | collective-permute-start | bytes 9043976 | tf_op jit(solution)/shard_map/ppermute | solution.py:682
  925.8 93.8 %collective-permute-start.18 = (f32[368,16,128]{2,1,0:T(8,128)}, f32[368,16,128]{2,1,0:T(8,128)S(1)}, u32[]{:S(2)}, u32[]{:S(2)}) collective-permute-start(f32[368,16,128]{2,1,0:T(8,128)} %get-tuple-element.449), channel_id=1, source_target_pairs={{2,0}} | collective-permute-start | bytes 9043976 | tf_op jit(solution)/shard_map/ppermute | solution.py:682
  1000.1 57.9 %collective-permute-start.23 = (f32[368,16,128]{2,1,0:T(8,128)}, f32[368,16,128]{2,1,0:T(8,128)}, u32[]{:S(2)}, u32[]{:S(2)}) collective-permute-start(f32[368,16,128]{2,1,0:T(8,128)} %collective-permute-done.8), channel_id=1, source_target_pairs={{3,0}} | collective-permute-start | bytes 9043976 | tf_op jit(solution)/shard_map/ppermute | solution.py:1063
  1018.2 53.4 %collective-permute-start.15 = (f32[368,16,128]{2,1,0:T(8,128)}, f32[368,16,128]{2,1,0:T(8,128)}, u32[]{:S(2)}, u32[]{:S(2)}) collective-permute-start(f32[368,16,128]{2,1,0:T(8,128)} %get-tuple-element.397), channel_id=1, source_target_pairs={{6,0}} | collective-permute-start | bytes 9043976 | tf_op jit(solution)/shard_map/ppermute | solution.py:682
  1019.5 115.5 %collective-permute-start.14 = (f32[368,16,128]{2,1,0:T(8,128)}, f32[368,16,128]{2,1,0:T(8,128)}, u32[]{:S(2)}, u32[]{:S(2)}) collective-permute-start(f32[368,16,128]{2,1,0:T(8,128)} %get-tuple-element.397), channel_id=1, source_target_pairs={{5,0}} | collective-permute-start | bytes 9043976 | tf_op jit(solution)/shard_map/ppermute | solution.py:682
  1020.8 115.4 %collective-permute-start.13 = (f32[368,16,128]{2,1,0:T(8,128)}, f32[368,16,128]{2,1,0:T(8,128)}, u32[]{:S(2)}, u32[]{:S(2)}) collective-permute-start(f32[368,16,128]{2,1,0:T(8,128)} %get-tuple-element.397), channel_id=1, source_target_pairs={{4,0}} | collective-permute-start | bytes 9043976 | tf_op jit(solution)/shard_map/ppermute | solution.py:682
  1022.2 115.4 %collective-permute-start.12 = (f32[368,16,128]{2,1,0:T(8,128)}, f32[368,16,128]{2,1,0:T(8,128)}, u32[]{:S(2)}, u32[]{:S(2)}) collective-permute-start(f32[368,16,128]{2,1,0:T(8,128)} %get-tuple-element.397), channel_id=1, source_target_pairs={{3,0}} | collective-permute-start | bytes 9043976 | tf_op jit(solution)/shard_map/ppermute | solution.py:682
  1071.6 245.9 %collective-permute-start.24 = (f32[2,256,1792]{2,1,0:T(8,128)}, f32[2,256,1792]{2,1,0:T(8,128)}, u32[]{:S(2)}, u32[]{:S(2)}) collective-permute-start(f32[2,256,1792]{2,1,0:T(8,128)} %get-tuple-element.457), channel_id=1, source_target_pairs={{0,2},{1,3},{2,0},{3,1},{4,6},{5,7},{6,4},{7,5}} | collective-permute-start | bytes 11010056 | tf_op jit(solution)/shard_map/ppermute | solution.py:810
  1071.6 249.7 %collective-permute-start.25 = (f32[2,256,1920]{2,1,0:T(8,128)}, f32[2,256,1920]{2,1,0:T(8,128)}, u32[]{:S(2)}, u32[]{:S(2)}) collective-permute-start(f32[2,256,1920]{2,1,0:T(8,128)} %slice.167), channel_id=1, source_target_pairs={{0,4},{1,5},{2,6},{3,7},{4,0},{5,1},{6,2},{7,3}} | collective-permute-start | bytes 11796488 | tf_op jit(solution)/shard_map/ppermute | solution.py:810
  1135.0 81.7 %collective-permute-start.11 = (f32[368,16,128]{2,1,0:T(8,128)}, f32[368,16,128]{2,1,0:T(8,128)}, u32[]{:S(2)}, u32[]{:S(2)}) collective-permute-start(f32[368,16,128]{2,1,0:T(8,128)} %get-tuple-element.397), channel_id=1, source_target_pairs={{2,0}} | collective-permute-start | bytes 9043976 | tf_op jit(solution)/shard_map/ppermute | solution.py:682
  1136.3 80.4 %collective-permute-start.10 = (f32[368,16,128]{2,1,0:T(8,128)}, f32[368,16,128]{2,1,0:T(8,128)}, u32[]{:S(2)}, u32[]{:S(2)}) collective-permute-start(f32[368,16,128]{2,1,0:T(8,128)} %get-tuple-element.397), channel_id=1, source_target_pairs={{1,0}} | collective-permute-start | bytes 9043976 | tf_op jit(solution)/shard_map/ppermute | solution.py:682
  1137.6 79.1 %collective-permute-start.16 = (f32[368,16,128]{2,1,0:T(8,128)}, f32[368,16,128]{2,1,0:T(8,128)}, u32[]{:S(2)}, u32[]{:S(2)}) collective-permute-start(f32[368,16,128]{2,1,0:T(8,128)} %collective-permute-done), channel_id=1, source_target_pairs={{3,0}} | collective-permute-start | bytes 9043976 | tf_op jit(solution)/shard_map/ppermute | solution.py:1044
  1325.3 24.7 %collective-permute-start.26 = (f32[256,1920]{1,0:T(8,128)S(1)}, f32[256,1920]{1,0:T(8,128)S(1)}, u32[]{:S(2)}, u32[]{:S(2)}) collective-permute-start(f32[256,1920]{1,0:T(8,128)S(1)} %slice_bitcast_fusion.8), channel_id=1, source_target_pairs={{0,2},{1,3},{2,0},{3,1},{4,6},{5,7},{6,4},{7,5}} | collective-permute-start | bytes 5898248 | tf_op jit(solution)/shard_map/ppermute | solution.py:810
  (62 other events, 2681.7 us)
Sparse Core Ops, SparseCore 0:
  11.8 5.4 sort.11.cloned.1.call-done
  (1 shorter events, 0.0 us)
Sparse Core Ops, SparseCore 1:
  18.4 116.4 all-gather.2
  221.0 68.5 all-gather.4
  643.8 279.7 reduce-scatter.1
